TPU v7x, 32 devices: a whole 2x2x4 slice. The times are simulated.
32 devices in a mesh: expert: 8 (over z, y), gate: 4 (over x, core).
Axes of the slice: x: 2, y: 2, z: 4, core: 2. Of those that a mesh axis runs over, the one named last changes fastest.
Arguments:
- samples: bfloat16 [6144, 4096], P('expert', 'gate'), may hold values from -4 to 4
- gate_weight: bfloat16 [4096, 32], P('gate'), may hold values from -1 to 1
- expert_ids: int32 [6144, 2], P('expert'), may hold values from 0 to 31, all different within a row; in each aligned block of 768 rows (0 to 767, 768 to 1535, ...) at most 96 rows name the same one
- pad_mask: int32 [6144], P('expert'), may hold values 0 or 1
- up_weight: bfloat16 [32, 4096, 1024], P(('expert', 'gate')), may hold values from -0.09375 to 0.09375
- down_weight: bfloat16 [32, 1024, 1024], P(('expert', 'gate')), may hold values from -0.1875 to 0.1875
Outputs:
- combined: bfloat16 [6144, 1024], P('expert', 'gate')
Inputs may be any that keep to these rules, and one draw needn't show every extreme that they name: `expert_ids`: each sample names two different experts; among the 768 samples of one index of expert no expert is named more than 96 times, a bound that some block reaches.
All inputs are finite; a program needn't handle non-finite values. No bound on the sum of `pad_mask` on one device may be relied on, other than what follows from the above.
Results may differ from a plain program's by a relative error of at most 0.0057.
Values may be sent and summed in bfloat16 or wider, within the bound.
A program may use at most 128 MiB of HBM per device.

v0:
```python
import functools

import jax
import jax.numpy as jnp
from jax import lax
from jax.experimental import pallas as pl
from jax.experimental.pallas import tpu as pltpu
from jax.sharding import PartitionSpec as P


MESH = pl.DeviceIdType.MESH
CHUNKS = 4
SIDES = 2


def routing(expert_ids, expert_count):
    row_count = expert_ids.shape[0]
    lanes = jnp.arange(expert_count, dtype=jnp.int32)[None, :]
    first = expert_ids[:, 0:1] == lanes
    second = expert_ids[:, 1:2] == lanes
    member = first | second
    rows = jnp.arange(row_count, dtype=jnp.int32)
    lower = (rows[:, None] > rows[None, :]).astype(jnp.bfloat16)
    before = jnp.dot(lower, member.astype(jnp.bfloat16), preferred_element_type=jnp.float32)
    before = before.astype(jnp.int32)
    return first, second, member, before


def factors(logits, first, second, pad_mask, expert_count):
    top = jnp.max(logits, axis=1, keepdims=True)
    terms = jnp.exp(logits - top)
    scale = pad_mask.astype(jnp.float32)[:, None] / jnp.sum(terms, axis=1, keepdims=True)
    factor0 = expert_count * jnp.sum(jnp.where(first, terms, 0.0), axis=1, keepdims=True) * scale
    factor1 = expert_count * jnp.sum(jnp.where(second, terms, 0.0), axis=1, keepdims=True) * scale
    return factor0, factor1


def copied(source, target, sem):
    return pltpu.make_async_copy(source, target, sem)


def sent(source, target, send_sem, recv_sem, device):
    return pltpu.make_async_remote_copy(
        src_ref=source,
        dst_ref=target,
        send_sem=send_sem,
        recv_sem=recv_sem,
        device_id=device,
        device_id_type=MESH,
    )


def table(values, index):
    out = values[0]
    for k in range(1, len(values)):
        out = jnp.where(index == k, values[k], out)
    return out


def exchange_kernel(
    planes,
    gates,
    capacity,
    samples,
    place,
    gate_weight,
    up,
    down,
    ret,
    logits,
    blocks,
    places,
    onehot,
    dbuf,
    inc,
    upv,
    downv,
    hidden,
    obuf,
    own_sem,
    w_sem,
    zs_up,
    zs_down,
    zs_relay,
    zr,
    ps,
    pr,
    rs,
    rr,
    ms,
    mr,
    gs,
    gr,
    l_sem,
):
    chunks = CHUNKS
    local = SIDES * gates
    e = lax.axis_index("expert")
    g = lax.axis_index("gate")
    z = e // SIDES
    y = lax.rem(e, SIDES)
    mine = y * gates + g
    me = e * gates + g
    total = planes * local
    rows = blocks.shape[2]
    width = blocks.shape[3]
    slots = local * capacity

    own = [
        copied(samples.at[:, pl.ds(c * width, width)], blocks.at[z, c], own_sem.at[c])
        for c in range(chunks)
    ]
    for copy in own:
        copy.start()
    weights = (copied(up.at[0], upv, w_sem.at[0]), copied(down.at[0], downv, w_sem.at[1]))
    kept = copied(place.at[pl.ds(z * local, local)], places.at[z], l_sem)
    kept.start()

    barrier = pltpu.get_barrier_semaphore()

    def greet(d, carry):
        t = lax.rem(me + d, total)
        pl.semaphore_signal(
            barrier, inc=1, device_id=(t // gates, lax.rem(t, gates)), device_id_type=MESH
        )
        return carry

    lax.fori_loop(1, total, greet, 0)
    pl.semaphore_wait(barrier, total - 1)

    routes = []
    for d in range(1, planes):
        j = lax.rem(z + d, planes)
        routes.append(
            sent(
                place.at[pl.ds(j * local, local)],
                places.at[z],
                ms.at[d - 1],
                mr.at[z],
                (j * SIDES + y, g),
            )
        )
        routes[-1].start()
    up_ok = z + 1 < planes
    down_ok = z >= 1

    def shift(j, c, sem, step):
        return sent(
            blocks.at[j, c], blocks.at[j, c], sem, zr.at[j, c], ((z + step) * SIDES + y, g)
        )

    for c in range(chunks):
        own[c].wait()

        @pl.when(up_ok)
        def _():
            shift(z, c, zs_up.at[c], 1).start()

        @pl.when(down_ok)
        def _():
            shift(z, c, zs_down.at[c], -1).start()

    for copy in weights:
        copy.start()
    partial = 0.0
    for c in range(chunks):
        partial += lax.dot_general(
            gate_weight[:, c * width : (c + 1) * width],
            blocks[z, c],
            (((1,), (1,)), ((), ())),
            preferred_element_type=jnp.float32,
        )
    logits[g] = partial
    kept.wait()
    gate_routes = []
    for d in range(1, gates):
        t = lax.rem(g + d, gates)
        gate_routes.append(sent(logits.at[g], logits.at[g], gs.at[d - 1], gr.at[d - 1], (e, t)))

    orders = [sorted(range(planes), key=lambda j: (abs(j - k), j)) for k in range(planes)]

    def block_at(p):
        return table([table(order, p) for order in orders], z)

    def relay_up(j):
        return (j < z) & up_ok

    def relay_down(j):
        return (j > z) & down_ok

    items = planes * chunks

    def held_back(j):
        return up_ok & down_ok & ((j == 0) | (j == planes - 1))

    def give_back(j):
        def hand(i, carry):
            side, k = i // gates, lax.rem(i, gates)
            block = obuf.at[j, k, pl.ds(side * capacity, capacity)]
            away = (j != z) | (i != mine)

            @pl.when(away)
            def _():
                sent(block, ret.at[me], rs, rr.at[me], (j * SIDES + side, k)).start()

            @pl.when(jnp.logical_not(away))
            def _():
                copied(block, ret.at[me], rr.at[me]).start()

            return carry

        lax.fori_loop(0, local, hand, 0)

    def item(t):
        u = t - chunks
        in_turn = up_ok & down_ok & (u >= 0) & (u < 2 * chunks)
        p = jnp.where(in_turn, 1 + lax.rem(u + 2 * chunks, 2), t // chunks)
        return p, jnp.where(in_turn, u // 2, lax.rem(t, chunks))

    def dispatch(t):
        p, c = item(t)
        j = block_at(p)
        lane = lax.rem(p, 2)

        @pl.when(j != z)
        def _():
            copied(blocks.at[j, c], blocks.at[j, c], zr.at[j, c]).wait()

            @pl.when(relay_up(j))
            def _():
                shift(j, c, zs_relay.at[j, c], 1).start()

            @pl.when(relay_down(j))
            def _():
                shift(j, c, zs_relay.at[j, c], -1).start()

        @pl.when(c == 0)
        def _():
            @pl.when(j != z)
            def _():
                copied(places.at[j], places.at[j], mr.at[j]).wait()

            ranks = lax.broadcasted_iota(jnp.int32, (capacity, rows), 0).astype(jnp.float32)
            for i in range(local):
                line = places[j, i : i + 1, :]
                onehot[lane, i * capacity : (i + 1) * capacity, :] = jnp.where(
                    line == ranks, 1.0, 0.0
                ).astype(jnp.bfloat16)

        half = slots // 2
        for h in range(2):
            picked = jnp.dot(
                onehot[lane, h * half : (h + 1) * half, :],
                blocks[j, c],
                preferred_element_type=jnp.float32,
            ).astype(jnp.bfloat16)
            dbuf[j, c, h * half : (h + 1) * half, :] = picked

        def give(d, carry):
            i = lax.rem(mine + d, local)
            sent(
                dbuf.at[j, c, pl.ds(i * capacity, capacity)],
                inc.at[j, c, g, pl.ds(y * capacity, capacity)],
                ps,
                pr.at[j, c],
                (z * SIDES + i // gates, lax.rem(i, gates)),
            ).start()
            return carry

        lax.fori_loop(1, local, give, 0)
        copied(
            dbuf.at[j, c, pl.ds(mine * capacity, capacity)],
            inc.at[j, c, g, pl.ds(y * capacity, capacity)],
            pr.at[j, c],
        ).start()

    def expert(t):
        p, c = item(t)
        j = block_at(p)
        lane = lax.rem(p, 2)
        copied(inc.at[j, c], inc.at[j, c], pr.at[j, c]).wait()
        share = width * chunks
        tile = 256
        for n in range(hidden.shape[2] // tile):
            cols = slice(n * tile, (n + 1) * tile)
            acc = jnp.zeros((SIDES * capacity, tile), jnp.float32)
            for k in range(gates):
                start = pl.multiple_of(k * share + c * width, width)
                acc += jnp.dot(
                    inc[j, c, k], upv[pl.ds(start, width), cols], preferred_element_type=jnp.float32
                )

            @pl.when(c == 0)
            def _():
                hidden[lane, :, cols] = acc

            @pl.when(c != 0)
            def _():
                hidden[lane, :, cols] += acc

        @pl.when(c == chunks - 1)
        def _():
            active = jnp.maximum(hidden[lane], 0.0).astype(jnp.bfloat16)
            out_width = downv.shape[1] // gates
            for k in range(gates):
                out = jnp.dot(
                    active,
                    downv[:, k * out_width : (k + 1) * out_width],
                    preferred_element_type=jnp.float32,
                ).astype(jnp.bfloat16)
                obuf[j, k] = out

            @pl.when(jnp.logical_not(held_back(j)))
            def _():
                give_back(j)

    def step(t, carry):
        @pl.when(t < items)
        def _():
            dispatch(t)

        @pl.when(t == 1)
        def _():
            for copy in gate_routes:
                copy.start()
            for copy in weights:
                copy.wait()

        @pl.when(t >= 1)
        def _():
            expert(t - 1)

        return carry

    lax.fori_loop(0, items + 1, step, 0)

    for c in range(chunks):

        @pl.when(up_ok)
        def _():
            shift(z, c, zs_up.at[c], 1).wait_send()

        @pl.when(down_ok)
        def _():
            shift(z, c, zs_down.at[c], -1).wait_send()

    def relayed(t, carry):
        j, c = t // chunks, lax.rem(t, chunks)

        @pl.when(relay_up(j) | relay_down(j))
        def _():
            copied(blocks.at[j, c], blocks.at[j, c], zs_relay.at[j, c]).wait()

        return carry

    lax.fori_loop(0, items, relayed, 0)

    @pl.when(up_ok & down_ok)
    def _():
        for j in (0, planes - 1):
            give_back(j)

    for copy in routes + gate_routes:
        copy.wait_send()
    for copy in gate_routes:
        copy.wait_recv()
    given = dbuf.at[:, :, pl.ds(0, slots - capacity)]
    copied(given, given, ps).wait()
    handed = ret.at[pl.ds(0, total - 1)]
    copied(handed, handed, rs).wait()

    def arrived(i, carry):
        copied(ret.at[i], ret.at[i], rr.at[i]).wait()
        return carry

    lax.fori_loop(0, total, arrived, 0)


def exchange(samples, place, gate_weight, up, down, planes, gates, capacity):
    rows, share = samples.shape
    local = SIDES * gates
    total = planes * local
    width = share // CHUNKS
    depth, inner = up.shape[1:]
    outer = down.shape[2]
    out_width = outer // gates
    bf16, f32 = jnp.bfloat16, jnp.float32
    dma = pltpu.SemaphoreType.DMA
    vmem = pl.BlockSpec(memory_space=pltpu.VMEM)
    hbm = pl.BlockSpec(memory_space=pl.ANY)
    return pl.pallas_call(
        functools.partial(exchange_kernel, planes, gates, capacity),
        out_shape=(
            jax.ShapeDtypeStruct((total, capacity, out_width), bf16),
            jax.ShapeDtypeStruct((gates, total, rows), f32),
        ),
        in_specs=[hbm, vmem, vmem, hbm, hbm],
        out_specs=(vmem, vmem),
        scratch_shapes=[
            pltpu.VMEM((planes, CHUNKS, rows, width), bf16),
            pltpu.VMEM((planes, local, rows), f32),
            pltpu.VMEM((2, local * capacity, rows), bf16),
            pltpu.VMEM((planes, CHUNKS, local * capacity, width), bf16),
            pltpu.VMEM((planes, CHUNKS, gates, SIDES * capacity, width), bf16),
            pltpu.VMEM((depth, inner), bf16),
            pltpu.VMEM((inner, outer), bf16),
            pltpu.VMEM((2, SIDES * capacity, inner), f32),
            pltpu.VMEM((planes, gates, SIDES * capacity, out_width), bf16),
            dma((CHUNKS,)),
            dma((2,)),
            dma((CHUNKS,)),
            dma((CHUNKS,)),
            dma((planes, CHUNKS)),
            dma((planes, CHUNKS)),
            dma,
            dma((planes, CHUNKS)),
            dma,
            dma((total,)),
            dma((planes,)),
            dma((planes,)),
            dma((gates,)),
            dma((gates,)),
            dma,
        ],
        compiler_params=pltpu.CompilerParams(
            collective_id=0, has_side_effects=True, vmem_limit_bytes=56 << 20
        ),
    )(samples, place, gate_weight, up, down)


def combine(returned, expert_ids, first, second, before, factor0, factor1, capacity):
    slots = jnp.arange(returned.shape[0], dtype=jnp.int32)[None, :]
    mixed = 0.0
    for k, (chosen, factor) in enumerate(((first, factor0), (second, factor1))):
        rank = jnp.sum(jnp.where(chosen, before, 0), axis=1, keepdims=True)
        position = expert_ids[:, k : k + 1] * capacity + rank
        pick = (position == slots).astype(jnp.bfloat16)
        mixed += factor * jnp.dot(pick, returned, preferred_element_type=jnp.float32)
    return mixed.astype(jnp.bfloat16)


def in_one_kernel(samples, gate_weight, expert_ids, pad_mask, up_weight, down_weight):
    group_count = lax.axis_size("expert")
    gate_count = lax.axis_size("gate")
    expert_count = group_count * gate_count
    capacity = 4 * samples.shape[0] // expert_count
    first, second, member, before = routing(expert_ids, expert_count)
    place = jnp.where(member, before, -1).T.astype(jnp.float32)
    returned, logits = exchange(
        samples,
        place,
        gate_weight.T,
        up_weight,
        down_weight,
        group_count // SIDES,
        gate_count,
        capacity,
    )
    returned = returned.reshape(expert_count * capacity, -1)
    logits = jnp.sum(logits, axis=0).T
    factor0, factor1 = factors(logits, first, second, pad_mask, expert_count)
    return combine(returned, expert_ids, first, second, before, factor0, factor1, capacity)


def fits(samples, up_weight, down_weight):
    group_count = lax.axis_size("expert")
    capacity = 4 * samples.shape[0] // (group_count * lax.axis_size("gate"))
    planes = group_count // SIDES
    held = 2 * (planes * samples.size * 3 + up_weight.size + down_weight.size)
    return group_count % SIDES == 0 and capacity % 16 == 0 and held < 40 << 20


def per_device(samples, gate_weight, expert_ids, pad_mask, up_weight, down_weight):
    if fits(samples, up_weight, down_weight):
        return in_one_kernel(
            samples, gate_weight, expert_ids, pad_mask, up_weight, down_weight
        )
    row_count, share = samples.shape
    group_count = lax.axis_size("expert")
    gate_count = lax.axis_size("gate")
    expert_count = group_count * gate_count
    capacity = 4 * row_count // expert_count
    partial = jnp.dot(samples, gate_weight, preferred_element_type=jnp.float32)
    logits = jnp.sum(lax.all_gather(partial, "gate"), axis=0)
    first, second, member, before = routing(expert_ids, expert_count)
    place = jnp.where(member, before, -1).T
    ranks = jnp.arange(capacity, dtype=jnp.int32)
    send = (place[:, None, :] == ranks[None, :, None]).astype(jnp.bfloat16)
    outgoing = jnp.dot(
        send.reshape(expert_count * capacity, row_count), samples, preferred_element_type=jnp.float32
    ).astype(jnp.bfloat16)
    incoming = lax.all_to_all(
        outgoing.reshape(expert_count, capacity, share),
        ("expert", "gate"),
        split_axis=0,
        concat_axis=0,
        tiled=True,
    ).reshape(group_count, gate_count, capacity, share)
    hidden = 0.0
    for g in range(gate_count):
        hidden += jnp.dot(
            incoming[:, g].reshape(group_count * capacity, share),
            up_weight[0, g * share : (g + 1) * share],
            preferred_element_type=jnp.float32,
        )
    active = jnp.maximum(hidden, 0.0).astype(jnp.bfloat16)
    expert_out = jnp.dot(active, down_weight[0], preferred_element_type=jnp.float32).astype(
        jnp.bfloat16
    )
    out_share = expert_out.shape[1] // gate_count
    outbound = expert_out.reshape(group_count, capacity, gate_count, out_share)
    outbound = outbound.transpose(0, 2, 1, 3).reshape(expert_count, capacity, out_share)
    returned = lax.all_to_all(
        outbound, ("expert", "gate"), split_axis=0, concat_axis=0, tiled=True
    ).reshape(expert_count * capacity, out_share)
    factor0, factor1 = factors(logits, first, second, pad_mask, expert_count)
    slots = jnp.arange(expert_count * capacity, dtype=jnp.int32)[None, :]
    mixed = 0.0
    for k, (chosen, factor) in enumerate(((first, factor0), (second, factor1))):
        rank = jnp.sum(jnp.where(chosen, before, 0), axis=1, keepdims=True)
        position = expert_ids[:, k : k + 1] * capacity + rank
        pick = (position == slots).astype(jnp.bfloat16)
        mixed += factor * jnp.dot(pick, returned, preferred_element_type=jnp.float32)
    return mixed.astype(jnp.bfloat16)


def solution(mesh):
    placed = (
        P("expert", "gate"),
        P("gate", None),
        P("expert", None),
        P("expert"),
        P(("expert", "gate"), None, None),
        P(("expert", "gate"), None, None),
    )
    return jax.shard_map(
        per_device, mesh=mesh, in_specs=placed, out_specs=P("expert", "gate"), check_vma=False
    )
```

profile of v0, /device:TPU:31, one launch (start us, length us, event | category | flops | bytes accessed | tf_op | source)
XLA Modules:
  0.0 153.1 jit_solution(13688522369328257385)
XLA Ops:
  0.0 0.8 slice_reduce_fusion.1
  0.8 1.0 fusion.12
  1.8 0.8 add_reduce_fusion.1
  2.6 0.0 copy-start
  2.6 143.6 %shard_map.64 = (bf16[32,96,256]{2,1,0:T(8,128)(2,1)}, f32[4,32,768]{2,1,0:T(8,128)}) custom-call(bf16[768,1024]{1,0:T(8,128)(2,1)} %samples.1, f32[32,768]{1,0:T(8,128)} %get-tuple-element.19.place, bf16[32,1024]{1,0:T(8,128)(2,1)} %bitcast.15, bf16[1,4096,1024]{2,1,0:T(8,128)(2,1)} %up.1, bf16[1,1024,1024]{2,1,0:T(8,128)(2,1)} %down.1), custom_call_target="tpu_custom_call" | custom-call | tf_op jit(solution)/shard_map/pallas_call | solution.py:391
  146.2 1.0 reduce_sum.54
  147.4 0.0 copy-done
  147.4 0.0 copy-start.1
  147.4 3.2 %fusion.5 = f32[768,256]{1,0:T(8,128)S(1)} fusion(bf16[3072,256]{1,0:T(8,128)(2,1)} %bitcast.16, s32[768]{0:T(1024)S(1)} %get-tuple-element.14, f32[768]{0:T(1024)S(1)} %get-tuple-element.18), kind=kOutput, calls=%fused_computation.8 | convolution fusion | flops 1210515456 | bytes 2365440 | tf_op jit(solution)/shard_map/dot_general | solution.py:438
  150.6 0.0 copy-done.1
  150.6 2.5 %fusion.8 = bf16[768,256]{1,0:T(8,128)(2,1)} fusion(f32[768,256]{1,0:T(8,128)S(1)} %fusion.5, bf16[3072,256]{1,0:T(8,128)(2,1)S(1)} %bitcast.17, s32[768]{0:T(1024)S(1)} %get-tuple-element.13, f32[768]{0:T(1024)S(1)} %get-tuple-element.17), kind=kOutput, calls=%fused_computation.11 | convolution fusion | flops 1210908672 | bytes 2758656 | tf_op jit(solution)/shard_map/dot_general | solution.py:438
  (5 shorter events, 0.1 us)
Async XLA Ops:
  2.6 144.7 %copy-start = (s32[768]{0:T(1024)S(1)}, s32[768]{0:T(1024)}, u32[]{:S(2)}) copy-start(s32[768]{0:T(1024)} %param.9) | copy-start | bytes 9220
  147.4 3.3 %copy-start.1 = (bf16[32,96,256]{2,1,0:T(8,128)(2,1)S(1)}, bf16[32,96,256]{2,1,0:T(8,128)(2,1)}, u32[]{:S(2)}) copy-start(bf16[32,96,256]{2,1,0:T(8,128)(2,1)} %get-tuple-element.8) | copy-start | bytes 4718596
where the time goes:
time: 153 us
  Pallas kernels  144 us (94%)
  matrix products  6.72 us (4%)
  other arithmetic  1.97 us (1%)
    pallas_call x1, Pallas kernels, exchange(): pl.pallas_call(functools.partial(exchange_kernel, planes, gates, capacity...  144 us
    dot_general x2, matrix products, combine(): jnp.dot(pick, returned, preferred_element_type=jnp.float32)  5.73 us

commit v1 on v0

v1 whole, which is shorter than its diff:
```python
import functools

import jax
import jax.numpy as jnp
from jax import lax
from jax.experimental import pallas as pl
from jax.experimental.pallas import tpu as pltpu
from jax.sharding import PartitionSpec as P


MESH = pl.DeviceIdType.MESH
CHUNKS = 4
SIDES = 2


def routing(expert_ids, expert_count):
    row_count = expert_ids.shape[0]
    lanes = jnp.arange(expert_count, dtype=jnp.int32)[None, :]
    first = expert_ids[:, 0:1] == lanes
    second = expert_ids[:, 1:2] == lanes
    member = first | second
    rows = jnp.arange(row_count, dtype=jnp.int32)
    lower = (rows[:, None] > rows[None, :]).astype(jnp.bfloat16)
    before = jnp.dot(lower, member.astype(jnp.bfloat16), preferred_element_type=jnp.float32)
    before = before.astype(jnp.int32)
    return first, second, member, before


def factors(logits, first, second, pad_mask, expert_count):
    top = jnp.max(logits, axis=1, keepdims=True)
    terms = jnp.exp(logits - top)
    scale = pad_mask.astype(jnp.float32)[:, None] / jnp.sum(terms, axis=1, keepdims=True)
    factor0 = expert_count * jnp.sum(jnp.where(first, terms, 0.0), axis=1, keepdims=True) * scale
    factor1 = expert_count * jnp.sum(jnp.where(second, terms, 0.0), axis=1, keepdims=True) * scale
    return factor0, factor1


def copied(source, target, sem):
    return pltpu.make_async_copy(source, target, sem)


def sent(source, target, send_sem, recv_sem, device):
    return pltpu.make_async_remote_copy(
        src_ref=source,
        dst_ref=target,
        send_sem=send_sem,
        recv_sem=recv_sem,
        device_id=device,
        device_id_type=MESH,
    )


def table(values, index):
    out = values[0]
    for k in range(1, len(values)):
        out = jnp.where(index == k, values[k], out)
    return out


ORDER = ((0, 0), (0, 1), (0, 2), (2, 0), (2, 1), (3, 0), (3, 1), (3, 2), (3, 3), (2, 2), (2, 3), (0, 3))


def exchange_kernel(
    gates,
    capacity,
    samples,
    ids,
    gate_weight,
    up,
    down,
    out,
    blocks,
    named,
    places,
    lower,
    onehot,
    dbuf,
    inc,
    upv,
    downv,
    hidden,
    obuf,
    logits,
    factor,
    edge_factor,
    ret,
    edge_ret,
    select,
    mixed,
    part,
    taken,
    own_sem,
    w_sem,
    raw_s,
    raw_r,
    id_s,
    id_r,
    ds,
    pr,
    rs,
    rr,
    er,
    gs,
    gr,
    fs,
    fr,
    ts,
    tr,
):
    chunks = CHUNKS
    local = SIDES * gates
    planes = blocks.shape[0]
    total = planes * local
    rows = blocks.shape[2]
    width = blocks.shape[3]
    slots = local * capacity
    e = lax.axis_index("expert")
    g = lax.axis_index("gate")
    z = e // SIDES
    y = lax.rem(e, SIDES)
    mine = y * gates + g
    me = e * gates + g
    low = z < planes // 2
    toward = jnp.where(low, 1, -1)
    near = jnp.where(low, 0, planes - 1)
    far = planes - 1 - near
    edge = z == near
    middle = jnp.logical_not(edge)
    mid = near + toward
    inner = z + toward

    def plane_of(rel):
        return table((mid, near, mid + toward, far), rel)

    own = [
        copied(samples.at[:, pl.ds(c * width, width)], blocks.at[z, c], own_sem.at[c])
        for c in range(chunks)
    ]
    for copy in own:
        copy.start()
    weights = (copied(up.at[0], upv, w_sem.at[0]), copied(down.at[0], downv, w_sem.at[1]))
    for copy in weights:
        copy.start()

    barrier = pltpu.get_barrier_semaphore()

    def greet(d, carry):
        t = lax.rem(me + d, total)
        pl.semaphore_signal(
            barrier, inc=1, device_id=(t // gates, lax.rem(t, gates)), device_id_type=MESH
        )
        return carry

    lax.fori_loop(1, total, greet, 0)

    earlier = lax.broadcasted_iota(jnp.int32, (rows, rows), 0)
    later = lax.broadcasted_iota(jnp.int32, (rows, rows), 1)
    lower[...] = jnp.where(earlier < later, 1.0, 0.0).astype(jnp.bfloat16)
    named[z] = ids[...]

    def end_index(rel):
        return jnp.where(rel == 0, planes, planes - 1 + rel)

    def prepare(j, rel):
        lanes = lax.broadcasted_iota(jnp.int32, (total, rows), 0)
        member = (named[j, 0:1, :] == lanes) | (named[j, 1:2, :] == lanes)
        flags = jnp.where(member, 1.0, 0.0).astype(jnp.bfloat16)
        before = jnp.dot(flags, lower[...], preferred_element_type=jnp.float32)
        places[j] = jnp.where(member, before, -1.0)
        ranks = lax.broadcasted_iota(jnp.int32, (capacity, rows), 0).astype(jnp.float32)

        def build(index, plane):
            def one(i, carry):
                line = places[j, pl.ds(plane * local + i, 1), :]
                onehot[index, pl.ds(pl.multiple_of(i * capacity, capacity), capacity), :] = (
                    jnp.where(line == ranks, 1.0, 0.0).astype(jnp.bfloat16)
                )
                return carry

            lax.fori_loop(0, local, one, 0)

        @pl.when(middle & (rel != 1))
        def _():
            build(end_index(rel), near)

        build(rel, z)

    own_rel = jnp.where(edge, 1, 0)
    prepare(z, own_rel)
    for copy in own:
        copy.wait()
    pl.semaphore_wait(barrier, total - 1)

    def ids_to(step, sem):
        return sent(named.at[z], named.at[z], sem, id_r.at[z], ((z + step) * SIDES + y, g))

    ids_to(toward, id_s.at[0]).start()

    @pl.when(edge)
    def _():
        ids_to(2 * toward, id_s.at[1]).start()

    def shift(j, c):
        return sent(
            blocks.at[j, c], blocks.at[j, c], raw_s.at[j, c], raw_r.at[j, c], (inner * SIDES + y, g)
        )

    for c in range(2):
        shift(z, c).start()

    @pl.when(edge)
    def _():
        for c in range(2, chunks):
            shift(z, c).start()

    gate_routes = []
    for d in range(1, gates):
        t = lax.rem(g + d, gates)
        gate_routes.append(sent(logits.at[g], logits.at[g], gs.at[d - 1], gr.at[d - 1], (e, t)))

    def listed(s):
        rel = table([rel for rel, c in ORDER], s)
        return rel, table([c for rel, c in ORDER], s)

    def dispatch(s, q):
        rel, c = listed(jnp.minimum(s, len(ORDER) - 1))
        second = q == 2
        rel = jnp.where(edge | (second & (s < 5)), 1, jnp.where(second, 0, rel))
        c = jnp.where(edge, s, jnp.where(second, jnp.where(s < 5, s - 1, chunks - 1), c))
        valid = jnp.where(
            edge,
            (q == 1) & (s < chunks),
            jnp.where(
                q == 0,
                s < len(ORDER),
                jnp.where(q == 1, s < len(ORDER) - 1, (s >= 1) & (s <= 5)),
            ),
        )
        fresh = middle & (((q == 0) & (rel >= 2)) | ((q == 2) & (rel == 1)))

        @pl.when(valid)
        def _():
            j = plane_of(rel)

            @pl.when(fresh)
            def _():
                copied(blocks.at[j, c], blocks.at[j, c], raw_r.at[j, c]).wait()

                @pl.when(rel == 1)
                def _():
                    shift(j, c).start()

                    @pl.when(c == chunks - 1)
                    def _():
                        for k in range(2, chunks):
                            shift(z, k).start()

                @pl.when(c == 0)
                def _():
                    copied(named.at[j], named.at[j], id_r.at[j]).wait()
                    prepare(j, rel)

            to_end = q == 0
            index = jnp.where(to_end, end_index(rel), rel)
            plane = jnp.where(to_end, near, z)
            half = slots // 2
            for h in range(2):
                picked = jnp.dot(
                    onehot[index, h * half : (h + 1) * half, :],
                    blocks[j, c],
                    preferred_element_type=jnp.float32,
                ).astype(jnp.bfloat16)
                dbuf[index, c, h * half : (h + 1) * half, :] = picked

            def give(d, carry):
                i = lax.rem(mine + d, local)
                piece = dbuf.at[index, c, pl.ds(i * capacity, capacity)]
                place = inc.at[j, c, g, pl.ds(y * capacity, capacity)]
                here = jnp.logical_not(to_end) & (d == 0)

                @pl.when(here)
                def _():
                    copied(piece, place, pr.at[j, c]).start()

                @pl.when(jnp.logical_not(here))
                def _():
                    sent(
                        piece,
                        place,
                        ds,
                        pr.at[j, c],
                        (plane * SIDES + i // gates, lax.rem(i, gates)),
                    ).start()

                return carry

            lax.fori_loop(0, local, give, 0)

    def give_back(j):
        ends = (j == 0) | (j == planes - 1)
        joined = ends & (j != z)
        plane = jnp.where(joined, jnp.where(j == 0, 1, planes - 2), j)

        def hand(i, carry):
            side, k = i // gates, lax.rem(i, gates)
            block = obuf.at[j, k, pl.ds(side * capacity, capacity)]
            here = (plane == z) & (i == mine)
            spot = pl.ds(mine * capacity, capacity)

            def hand_to(buffer, sem):
                @pl.when(here)
                def _():
                    copied(block, buffer.at[z, spot], sem.at[z]).start()

                @pl.when(jnp.logical_not(here))
                def _():
                    sent(
                        block, buffer.at[z, spot], rs, sem.at[z], (plane * SIDES + side, k)
                    ).start()

            @pl.when(joined)
            def _():
                hand_to(edge_ret, er)

            @pl.when(jnp.logical_not(joined))
            def _():
                hand_to(ret, rr)

            return carry

        lax.fori_loop(0, local, hand, 0)

    def expert(s, q):
        t = s - 1
        order = jnp.where(edge, jnp.maximum(t - chunks, 0), jnp.minimum(t, len(ORDER) - 1))
        rel, c = listed(order)
        second = q == 1
        first_own = edge & (t < chunks)
        rel = jnp.where(
            first_own, 1, jnp.where(second, jnp.where(t < 5, 1, 0), rel)
        )
        c = jnp.where(
            first_own, t, jnp.where(second, jnp.where(t < 5, t - 1, chunks - 1), c)
        )
        valid = jnp.where(
            edge,
            (q == 0) & (t >= 0) & (t < len(ORDER) + chunks),
            jnp.where(q == 0, (t >= 0) & (t < len(ORDER) - 1), (t >= 1) & (t <= 5)),
        )

        @pl.when(valid)
        def _():
            j = plane_of(rel)
            copied(inc.at[j, c], inc.at[j, c], pr.at[j, c]).wait()
            share = width * chunks
            tile = 256
            for n in range(hidden.shape[2] // tile):
                cols = slice(n * tile, (n + 1) * tile)
                acc = jnp.zeros((SIDES * capacity, tile), jnp.float32)
                for k in range(gates):
                    start = pl.multiple_of(k * share + c * width, width)
                    acc += jnp.dot(
                        inc[j, c, k],
                        upv[pl.ds(start, width), cols],
                        preferred_element_type=jnp.float32,
                    )

                @pl.when(c == 0)
                def _():
                    hidden[j, :, cols] = acc

                @pl.when(c != 0)
                def _():
                    hidden[j, :, cols] += acc

            @pl.when(c == chunks - 1)
            def _():
                active = jnp.maximum(hidden[j], 0.0).astype(jnp.bfloat16)
                out_width = downv.shape[1] // gates
                for k in range(gates):
                    obuf[j, k] = jnp.dot(
                        active,
                        downv[:, k * out_width : (k + 1) * out_width],
                        preferred_element_type=jnp.float32,
                    ).astype(jnp.bfloat16)
                give_back(j)

    edge_route = sent(factor, edge_factor, fs, fr, (inner * SIDES + y, g))

    def step(s, carry):
        def dispatch_one(q, carry):
            dispatch(s, q)
            return carry

        lax.fori_loop(0, 3, dispatch_one, 0)

        @pl.when(s == 0)
        def _():
            partial = 0.0
            for c in range(chunks):
                partial += lax.dot_general(
                    gate_weight[:, c * width : (c + 1) * width],
                    blocks[z, c],
                    (((1,), (1,)), ((), ())),
                    preferred_element_type=jnp.float32,
                )
            logits[g] = partial
            for copy in gate_routes:
                copy.start()
            for copy in weights:
                copy.wait()

        @pl.when(s == 2)
        def _():
            for copy in gate_routes:
                copy.wait_recv()
            summed = logits[0]
            for k in range(1, gates):
                summed += logits[k]
            top = jnp.max(summed, axis=0, keepdims=True)
            terms = jnp.exp(summed - top)
            mask = ids[2:3, :].astype(jnp.float32)
            scale = mask / jnp.sum(terms, axis=0, keepdims=True)
            factor[...] = total * terms * scale

            @pl.when(edge)
            def _():
                edge_route.start()

        def expert_one(q, carry):
            expert(s, q)
            return carry

        lax.fori_loop(0, 2, expert_one, 0)
        return carry

    lax.fori_loop(0, len(ORDER) + chunks + 1, step, 0)

    def join(j, p, weight, returned, sem, index, first):
        ranks = lax.broadcasted_iota(jnp.int32, (capacity, rows), 0).astype(jnp.float32)

        def one(i, carry):
            line = places[j, pl.ds(p * local + i, 1), :]
            scale = weight[pl.ds(p * local + i, 1), :]
            select[pl.ds(pl.multiple_of(i * capacity, capacity), capacity), :] = jnp.where(
                line == ranks, scale, 0.0
            ).astype(jnp.bfloat16)
            return carry

        lax.fori_loop(0, local, one, 0)
        copied(returned.at[p], returned.at[p], sem.at[p]).wait()
        found = lax.dot_general(
            select[...],
            returned[p],
            (((0,), (0,)), ((), ())),
            preferred_element_type=jnp.float32,
        )

        @pl.when(first)
        def _():
            mixed[index] = found

        @pl.when(jnp.logical_not(first))
        def _():
            mixed[index] += found

    part_route = sent(part, taken, ts, tr, (near * SIDES + y, g))

    @pl.when(middle)
    def _():
        copied(edge_factor, edge_factor, fr).wait()

        def for_edge(k, carry):
            p = table((mid, mid + toward, far), k)
            join(near, p, edge_factor, edge_ret, er, 0, k == 0)
            return carry

        lax.fori_loop(0, planes - 1, for_edge, 0)
        part[...] = mixed[0].astype(jnp.bfloat16)
        part_route.start()

    def for_own(k, carry):
        p = jnp.where(edge, z, table((mid, mid + toward, far, near), k))
        join(z, p, factor, ret, rr, 1, k == 0)
        return carry

    lax.fori_loop(0, jnp.where(edge, 1, planes), for_own, 0)

    @pl.when(edge)
    def _():
        copied(taken, taken, tr).wait()
        out[...] = (mixed[1] + taken[...].astype(jnp.float32)).astype(jnp.bfloat16)

    @pl.when(middle)
    def _():
        out[...] = mixed[1].astype(jnp.bfloat16)
        part_route.wait_send()

    for copy in gate_routes:
        copy.wait_send()
    ids_to(toward, id_s.at[0]).wait_send()
    for c in range(chunks):
        shift(z, c).wait_send()
    handed = ret.at[pl.ds(0, planes - 1)]
    within = dbuf.at[0, :, pl.ds(0, slots - capacity)]
    piece = ret.at[0, pl.ds(0, (local - 2) * capacity)]
    last = ret.at[0, pl.ds(0, capacity)]
    copied(handed, handed, rs).wait()
    copied(piece, piece, rs).wait()
    copied(within, within, ds).wait()

    @pl.when(edge)
    def _():
        copied(last, last, rs).wait()
        ids_to(2 * toward, id_s.at[1]).wait_send()
        edge_route.wait_send()

    @pl.when(middle)
    def _():
        for c in range(chunks):
            shift(near, c).wait_send()
        others = dbuf.at[pl.ds(0, planes - 1), :, pl.ds(0, slots - capacity)]
        copied(others, others, ds).wait()
        ahead = dbuf.at[pl.ds(planes, planes - 1)]
        copied(ahead, ahead, ds).wait()


def exchange(samples, ids, gate_weight, up, down, planes, gates, capacity):
    rows, share = samples.shape
    local = SIDES * gates
    total = planes * local
    width = share // CHUNKS
    depth, inner = up.shape[1:]
    outer = down.shape[2]
    out_width = outer // gates
    bf16, f32 = jnp.bfloat16, jnp.float32
    dma = pltpu.SemaphoreType.DMA
    vmem = pl.BlockSpec(memory_space=pltpu.VMEM)
    hbm = pl.BlockSpec(memory_space=pl.ANY)
    slots = local * capacity
    kinds = 2 * planes - 1
    return pl.pallas_call(
        functools.partial(exchange_kernel, gates, capacity),
        out_shape=jax.ShapeDtypeStruct((rows, out_width), bf16),
        in_specs=[hbm, vmem, vmem, hbm, hbm],
        out_specs=vmem,
        scratch_shapes=[
            pltpu.VMEM((planes, CHUNKS, rows, width), bf16),
            pltpu.VMEM((planes,) + ids.shape, jnp.int32),
            pltpu.VMEM((planes, total, rows), f32),
            pltpu.VMEM((rows, rows), bf16),
            pltpu.VMEM((kinds, slots, rows), bf16),
            pltpu.VMEM((kinds, CHUNKS, slots, width), bf16),
            pltpu.VMEM((planes, CHUNKS, gates, SIDES * capacity, width), bf16),
            pltpu.VMEM((depth, inner), bf16),
            pltpu.VMEM((inner, outer), bf16),
            pltpu.VMEM((planes, SIDES * capacity, inner), f32),
            pltpu.VMEM((planes, gates, SIDES * capacity, out_width), bf16),
            pltpu.VMEM((gates, total, rows), f32),
            pltpu.VMEM((total, rows), f32),
            pltpu.VMEM((total, rows), f32),
            pltpu.VMEM((planes, slots, out_width), bf16),
            pltpu.VMEM((planes, slots, out_width), bf16),
            pltpu.VMEM((slots, rows), bf16),
            pltpu.VMEM((2, rows, out_width), f32),
            pltpu.VMEM((rows, out_width), bf16),
            pltpu.VMEM((rows, out_width), bf16),
            dma((CHUNKS,)),
            dma((2,)),
            dma((planes, CHUNKS)),
            dma((planes, CHUNKS)),
            dma((2,)),
            dma((planes,)),
            dma,
            dma((planes, CHUNKS)),
            dma,
            dma((planes,)),
            dma((planes,)),
            dma((gates,)),
            dma((gates,)),
            dma,
            dma,
            dma,
            dma,
        ],
        compiler_params=pltpu.CompilerParams(
            collective_id=0, has_side_effects=True, vmem_limit_bytes=63 << 20
        ),
    )(samples, ids, gate_weight, up, down)


def in_one_kernel(samples, gate_weight, expert_ids, pad_mask, up_weight, down_weight):
    group_count = lax.axis_size("expert")
    gate_count = lax.axis_size("gate")
    expert_count = group_count * gate_count
    capacity = 4 * samples.shape[0] // expert_count
    ids = jnp.concatenate([expert_ids.T, pad_mask[None, :]], axis=0)
    ids = jnp.pad(ids, ((0, 8 - ids.shape[0]), (0, 0)))
    return exchange(
        samples,
        ids,
        gate_weight.T,
        up_weight,
        down_weight,
        group_count // SIDES,
        gate_count,
        capacity,
    )


def fits(samples, up_weight, down_weight):
    group_count = lax.axis_size("expert")
    capacity = 4 * samples.shape[0] // (group_count * lax.axis_size("gate"))
    planes = group_count // SIDES
    held = 2 * (planes * samples.size * 3 + up_weight.size + down_weight.size)
    return planes == 4 and group_count % SIDES == 0 and capacity % 16 == 0 and held < 40 << 20


def per_device(samples, gate_weight, expert_ids, pad_mask, up_weight, down_weight):
    if fits(samples, up_weight, down_weight):
        return in_one_kernel(
            samples, gate_weight, expert_ids, pad_mask, up_weight, down_weight
        )
    row_count, share = samples.shape
    group_count = lax.axis_size("expert")
    gate_count = lax.axis_size("gate")
    expert_count = group_count * gate_count
    capacity = 4 * row_count // expert_count
    partial = jnp.dot(samples, gate_weight, preferred_element_type=jnp.float32)
    logits = jnp.sum(lax.all_gather(partial, "gate"), axis=0)
    first, second, member, before = routing(expert_ids, expert_count)
    place = jnp.where(member, before, -1).T
    ranks = jnp.arange(capacity, dtype=jnp.int32)
    send = (place[:, None, :] == ranks[None, :, None]).astype(jnp.bfloat16)
    outgoing = jnp.dot(
        send.reshape(expert_count * capacity, row_count), samples, preferred_element_type=jnp.float32
    ).astype(jnp.bfloat16)
    incoming = lax.all_to_all(
        outgoing.reshape(expert_count, capacity, share),
        ("expert", "gate"),
        split_axis=0,
        concat_axis=0,
        tiled=True,
    ).reshape(group_count, gate_count, capacity, share)
    hidden = 0.0
    for g in range(gate_count):
        hidden += jnp.dot(
            incoming[:, g].reshape(group_count * capacity, share),
            up_weight[0, g * share : (g + 1) * share],
            preferred_element_type=jnp.float32,
        )
    active = jnp.maximum(hidden, 0.0).astype(jnp.bfloat16)
    expert_out = jnp.dot(active, down_weight[0], preferred_element_type=jnp.float32).astype(
        jnp.bfloat16
    )
    out_share = expert_out.shape[1] // gate_count
    outbound = expert_out.reshape(group_count, capacity, gate_count, out_share)
    outbound = outbound.transpose(0, 2, 1, 3).reshape(expert_count, capacity, out_share)
    returned = lax.all_to_all(
        outbound, ("expert", "gate"), split_axis=0, concat_axis=0, tiled=True
    ).reshape(expert_count * capacity, out_share)
    factor0, factor1 = factors(logits, first, second, pad_mask, expert_count)
    slots = jnp.arange(expert_count * capacity, dtype=jnp.int32)[None, :]
    mixed = 0.0
    for k, (chosen, factor) in enumerate(((first, factor0), (second, factor1))):
        rank = jnp.sum(jnp.where(chosen, before, 0), axis=1, keepdims=True)
        position = expert_ids[:, k : k + 1] * capacity + rank
        pick = (position == slots).astype(jnp.bfloat16)
        mixed += factor * jnp.dot(pick, returned, preferred_element_type=jnp.float32)
    return mixed.astype(jnp.bfloat16)


def solution(mesh):
    placed = (
        P("expert", "gate"),
        P("gate", None),
        P("expert", None),
        P("expert"),
        P(("expert", "gate"), None, None),
        P(("expert", "gate"), None, None),
    )
    return jax.shard_map(
        per_device, mesh=mesh, in_specs=placed, out_specs=P("expert", "gate"), check_vma=False
    )
```

time: 153 us -> 135 us (0.88)
  the two profiles are of different devices: /device:TPU:31 before, /device:TPU:15 now
where the time goes in v1:
time: 135 us; the launch traced here: 134 us
  Pallas kernels  131 us (97%)
  local copies, waits for them, and re-layouts  3.07 us (2%)
    pallas_call x1, Pallas kernels, exchange(): pl.pallas_call(functools.partial(exchange_kernel, gates, capacity), out_s...  131 us

profile of v1, /device:TPU:15, one launch (start us, length us, event | category | flops | bytes accessed | tf_op | source)
XLA Modules:
  0.0 134.3 jit_solution(11560112849053096529)
XLA Ops:
  0.0 0.7 broadcast_in_dim.3
  0.7 0.7 pad_add_fusion
  1.4 0.6 pad.4.ids
  2.0 130.5 %shard_map.64 = bf16[768,256]{1,0:T(8,128)(2,1)} custom-call(bf16[768,1024]{1,0:T(8,128)(2,1)} %samples.1, s32[8,768]{1,0:T(8,128)} %pad.4.ids, bf16[32,1024]{1,0:T(8,128)(2,1)} %bitcast.2, bf16[1,4096,1024]{2,1,0:T(8,128)(2,1)} %up.1, bf16[1,1024,1024]{2,1,0:T(8,128)(2,1)} %down.1), custom_call_target="tpu_custom_call" | custom-call | tf_op jit(solution)/shard_map/pallas_call | solution.py:542
  132.6 1.8 %copy.8 = bf16[768,256]{1,0:T(8,128)(2,1)} copy(bf16[768,256]{1,0:T(8,128)(2,1)} %shard_map.64) | data formatting | bytes 786432

commit v2 on v1

v2 whole, which is shorter than its diff:
```python
import functools

import jax
import jax.numpy as jnp
from jax import lax
from jax.experimental import pallas as pl
from jax.experimental.pallas import tpu as pltpu
from jax.sharding import PartitionSpec as P


MESH = pl.DeviceIdType.MESH
CHUNKS = 4
SIDES = 2
PARTS = 2


def routing(expert_ids, expert_count):
    row_count = expert_ids.shape[0]
    lanes = jnp.arange(expert_count, dtype=jnp.int32)[None, :]
    first = expert_ids[:, 0:1] == lanes
    second = expert_ids[:, 1:2] == lanes
    member = first | second
    rows = jnp.arange(row_count, dtype=jnp.int32)
    lower = (rows[:, None] > rows[None, :]).astype(jnp.bfloat16)
    before = jnp.dot(lower, member.astype(jnp.bfloat16), preferred_element_type=jnp.float32)
    before = before.astype(jnp.int32)
    return first, second, member, before


def factors(logits, first, second, pad_mask, expert_count):
    top = jnp.max(logits, axis=1, keepdims=True)
    terms = jnp.exp(logits - top)
    scale = pad_mask.astype(jnp.float32)[:, None] / jnp.sum(terms, axis=1, keepdims=True)
    factor0 = expert_count * jnp.sum(jnp.where(first, terms, 0.0), axis=1, keepdims=True) * scale
    factor1 = expert_count * jnp.sum(jnp.where(second, terms, 0.0), axis=1, keepdims=True) * scale
    return factor0, factor1


def copied(source, target, sem):
    return pltpu.make_async_copy(source, target, sem)


def sent(source, target, send_sem, recv_sem, device):
    return pltpu.make_async_remote_copy(
        src_ref=source,
        dst_ref=target,
        send_sem=send_sem,
        recv_sem=recv_sem,
        device_id=device,
        device_id_type=MESH,
    )


def table(values, index):
    out = values[0]
    for k in range(1, len(values)):
        out = jnp.where(index == k, values[k], out)
    return out


NONE, WAIT, END, LOCAL, EXPERT, LOGITS, FACTOR, JOIN_EDGE, JOIN, END_PART, EXPERT_PART, WEIGHTS = range(12)
OWN, EDGE, INNER, FAR = range(4)


def coded(*jobs):
    return [kind * 16 + rel * 4 + c for kind, rel, c in jobs]


MIDDLE_JOBS = coded(
    (END, OWN, 0),
    (LOGITS, OWN, 0),
    (LOCAL, OWN, 0),
    (LOCAL, OWN, 1),
    (LOCAL, OWN, 2),
    (LOCAL, OWN, 3),
    (END, OWN, 1),
    (WEIGHTS, OWN, 0),
    (EXPERT, OWN, 0),
    (FACTOR, OWN, 0),
    (WAIT, EDGE, 0),
    (LOCAL, EDGE, 0),
    (WAIT, INNER, 0),
    (END, INNER, 0),
    (LOCAL, INNER, 0),
    (EXPERT, OWN, 1),
    (EXPERT, OWN, 2),
    (WAIT, EDGE, 1),
    (LOCAL, EDGE, 1),
    (WAIT, INNER, 1),
    (END, INNER, 1),
    (LOCAL, INNER, 1),
    (EXPERT, OWN, 3),
    (EXPERT, EDGE, 0),
    (WAIT, EDGE, 2),
    (LOCAL, EDGE, 2),
    (WAIT, FAR, 0),
    (END, FAR, 0),
    (LOCAL, FAR, 0),
    (EXPERT, INNER, 0),
    (EXPERT, EDGE, 1),
    (WAIT, EDGE, 3),
    (LOCAL, EDGE, 3),
    (WAIT, FAR, 1),
    (END, FAR, 1),
    (LOCAL, FAR, 1),
    (EXPERT, INNER, 1),
    (WAIT, FAR, 2),
    (END, FAR, 2),
    (LOCAL, FAR, 2),
    (EXPERT, EDGE, 2),
    (WAIT, FAR, 3),
    (END, FAR, 3),
    (LOCAL, FAR, 3),
    (EXPERT, FAR, 0),
    (EXPERT, EDGE, 3),
    (EXPERT, FAR, 1),
    (WAIT, INNER, 2),
    (END, INNER, 2),
    (LOCAL, INNER, 2),
    (EXPERT, FAR, 2),
    (EXPERT, FAR, 3),
    (WAIT, INNER, 3),
    (END, INNER, 3),
    (LOCAL, INNER, 3),
    (END, OWN, 2),
    (END_PART, OWN, 0),
    (END_PART, OWN, 1),
    (EXPERT, INNER, 2),
    (EXPERT, INNER, 3),
    (JOIN_EDGE, OWN, 0),
    (JOIN_EDGE, INNER, 0),
    (JOIN_EDGE, FAR, 0),
    (JOIN, OWN, 0),
    (JOIN, INNER, 0),
    (JOIN, FAR, 0),
    (JOIN, EDGE, 0),
)
EDGE_JOBS = coded(
    (LOCAL, EDGE, 0),
    (LOGITS, EDGE, 0),
    (LOCAL, EDGE, 1),
    (LOCAL, EDGE, 2),
    (LOCAL, EDGE, 3),
    (WEIGHTS, EDGE, 0),
    (EXPERT, EDGE, 0),
    (FACTOR, EDGE, 0),
    (EXPERT, EDGE, 1),
    (EXPERT, OWN, 0),
    (EXPERT, EDGE, 2),
    (EXPERT, OWN, 1),
    (EXPERT, EDGE, 3),
    (EXPERT, INNER, 0),
    (EXPERT, INNER, 1),
    (EXPERT, FAR, 0),
    (EXPERT, FAR, 1),
    (EXPERT, FAR, 2),
    (EXPERT, FAR, 3),
    (EXPERT, INNER, 2),
    (EXPERT, INNER, 3),
    (EXPERT, OWN, 2),
    (EXPERT_PART, OWN, 0),
    (EXPERT_PART, OWN, 1),
    (JOIN, EDGE, 0),
)


def exchange_kernel(
    gates,
    capacity,
    samples,
    ids,
    pads,
    gate_weight,
    up,
    down,
    out,
    blocks,
    named,
    mask,
    gatev,
    places,
    lower,
    onehot,
    dbuf,
    inc,
    upv,
    downv,
    hidden,
    obuf,
    logits,
    factor,
    edge_factor,
    ret,
    edge_ret,
    select,
    mixed,
    part,
    taken,
    own_sem,
    w_sem,
    in_sem,
    raw_s,
    raw_r,
    id_s,
    id_r,
    ds,
    pr,
    ph,
    rs,
    rr,
    er,
    gs,
    gr,
    fs,
    fr,
    ts,
    tr,
):
    chunks = CHUNKS
    local = SIDES * gates
    planes = blocks.shape[0]
    total = planes * local
    rows = blocks.shape[2]
    width = blocks.shape[3]
    share = width * chunks
    slots = local * capacity
    few = capacity // PARTS
    bf16, f32 = jnp.bfloat16, jnp.float32
    e = lax.axis_index("expert")
    g = lax.axis_index("gate")
    z = e // SIDES
    y = lax.rem(e, SIDES)
    mine = y * gates + g
    low = z < planes // 2
    toward = jnp.where(low, 1, -1)
    near = jnp.where(low, 0, planes - 1)
    far = planes - 1 - near
    edge = z == near
    middle = jnp.logical_not(edge)
    mid = near + toward
    inner = z + toward

    def plane_of(rel):
        return table((mid, near, mid + toward, far), rel)

    def at(plane, i):
        return (plane * SIDES + i // gates, lax.rem(i, gates))

    barrier = pltpu.get_barrier_semaphore()

    def greet(d, carry):
        plane = z - 1 + d // local
        i = lax.rem(mine + d, local)

        @pl.when((plane >= 0) & (plane < planes) & (d != local))
        def _():
            pl.semaphore_signal(barrier, inc=1, device_id=at(plane, i), device_id_type=MESH)

        return carry

    with jax.named_scope("greet"):
        lax.fori_loop(0, 3 * local, greet, 0)
    greeted = jnp.where(edge, 2, 3) * local - 1

    inputs = (
        copied(ids, named.at[z], in_sem.at[0]),
        copied(pads, mask, in_sem.at[1]),
        copied(gate_weight, gatev, in_sem.at[2]),
    )
    for copy in inputs:
        copy.start()
    own = [
        copied(samples.at[:, pl.ds(c * width, width)], blocks.at[z, c], own_sem.at[c])
        for c in range(chunks)
    ]
    for copy in own:
        copy.start()
    weights = [copied(down.at[0], downv, w_sem.at[0])]
    for c in range(chunks):
        for k in range(gates):
            weights.append(
                copied(
                    up.at[0, pl.ds(k * share + c * width, width)],
                    upv.at[c, pl.ds(k * width, width)],
                    w_sem.at[1 + c * gates + k],
                )
            )

    earlier = lax.broadcasted_iota(jnp.int32, (rows, rows), 0)
    later = lax.broadcasted_iota(jnp.int32, (rows, rows), 1)
    with jax.named_scope("lower"):
        lower[...] = jnp.where(earlier < later, 1.0, 0.0).astype(bf16)

    def end_index(rel):
        return jnp.where(rel == OWN, planes, planes - 1 + rel)

    def prepare(j, rel):
        lanes = lax.broadcasted_iota(jnp.int32, (total, rows), 0)
        member = (named[j, 0:1, :] == lanes) | (named[j, 1:2, :] == lanes)
        flags = jnp.where(member, 1.0, 0.0).astype(bf16)
        before = jnp.dot(flags, lower[...], preferred_element_type=f32)
        places[j] = jnp.where(member, before, -1.0)
        ranks = lax.broadcasted_iota(jnp.int32, (capacity, rows), 0).astype(f32)

        def build(index, plane):
            def one(i, carry):
                line = places[j, pl.ds(plane * local + i, 1), :]
                found = jnp.where(line == ranks, 1.0, 0.0).astype(bf16)
                onehot[index, :, i] = found.reshape(PARTS, few, rows)
                return carry

            lax.fori_loop(0, local, one, 0)

        @pl.when(middle & (rel != EDGE))
        def _():
            build(end_index(rel), near)

        build(rel, z)

    with jax.named_scope("inputs"):
        for copy in inputs:
            copy.wait()
    with jax.named_scope("prepare"):
        prepare(z, jnp.where(edge, EDGE, OWN))
    with jax.named_scope("samples"):
        for copy in own:
            copy.wait()
    with jax.named_scope("barrier"):
        pl.semaphore_wait(barrier, greeted)

    def ids_on(j, sem):
        return sent(named.at[j], named.at[j], sem, id_r.at[j], at(inner, mine))

    def shift(j, c):
        return sent(
            blocks.at[j, c], blocks.at[j, c], raw_s.at[j, c], raw_r.at[j, c], at(inner, mine)
        )

    ids_on(z, id_s.at[0]).start()
    for c in range(2):
        shift(z, c).start()

    @pl.when(edge)
    def _():
        for c in range(2, chunks):
            shift(z, c).start()

    for copy in weights:
        copy.start()
    gate_routes = []
    for d in range(1, gates):
        t = lax.rem(g + d, gates)
        gate_routes.append(sent(logits.at[g], logits.at[g], gs.at[d - 1], gr.at[d - 1], (e, t)))
    edge_route = sent(factor, edge_factor, fs, fr, at(inner, mine))
    part_route = sent(part, taken, ts, tr, at(near, mine))

    def wait(j, rel, c):
        with jax.named_scope("wait_raw"):
            copied(blocks.at[j, c], blocks.at[j, c], raw_r.at[j, c]).wait()

        @pl.when(c == 0)
        def _():
            copied(named.at[j], named.at[j], id_r.at[j]).wait()

        @pl.when(rel == EDGE)
        def _():
            @pl.when(c == 0)
            def _():
                ids_on(j, id_s.at[1]).start()

            shift(j, c).start()

            @pl.when(c == chunks - 1)
            def _():
                for k in range(2, chunks):
                    shift(z, k).start()

        @pl.when(c == 0)
        def _():
            prepare(j, rel)

    def pick(index, part, j, c):
        dbuf[index, c, part] = (
            jnp.dot(
                onehot[index, part].reshape(local * few, rows),
                blocks[j, c],
                preferred_element_type=f32,
            )
            .astype(bf16)
            .reshape(local, few, width)
        )

    def dispatch(j, rel, c, to_end):
        index = jnp.where(to_end, end_index(rel), rel)
        plane = jnp.where(to_end, near, z)
        with jax.named_scope("pick"):
            for part in range(PARTS):
                pick(index, part, j, c)

        def give(d, carry):
            i = lax.rem(mine + d, local)
            piece = dbuf.at[index, c, :, i]
            place = inc.at[j, c, y, :, :, pl.ds(g * width, width)]
            here = jnp.logical_not(to_end) & (d == 0)

            @pl.when(here)
            def _():
                copied(piece, place, pr.at[j, c]).start()

            @pl.when(jnp.logical_not(here))
            def _():
                sent(piece, place, ds, pr.at[j, c], at(plane, i)).start()

            return carry

        lax.fori_loop(0, local, give, 0)

    def dispatch_part(part):
        c = chunks - 1
        pick(planes, part, z, c)

        def give(d, carry):
            i = lax.rem(mine + d, local)
            sent(
                dbuf.at[planes, c, part, i],
                inc.at[z, c, y, part, :, pl.ds(g * width, width)],
                ds,
                ph.at[part],
                at(near, i),
            ).start()
            return carry

        lax.fori_loop(0, local, give, 0)

    def give_back(j, part):
        ends = (j == 0) | (j == planes - 1)
        joined = ends & (j != z)
        plane = jnp.where(joined, jnp.where(j == 0, 1, planes - 2), j)

        def hand(d, carry):
            i = lax.rem(mine + d, local)
            side, k = i // gates, lax.rem(i, gates)
            here = (plane == z) & (d == 0)

            def hand_to(buffer, sem):
                if part is None:
                    block, spot = obuf.at[j, k, side], buffer.at[z, mine]
                else:
                    block, spot = obuf.at[j, k, side, part], buffer.at[z, mine, part]

                @pl.when(here)
                def _():
                    copied(block, spot, sem.at[z]).start()

                @pl.when(jnp.logical_not(here))
                def _():
                    sent(block, spot, rs, sem.at[z], at(plane, i)).start()

            @pl.when(joined)
            def _():
                hand_to(edge_ret, er)

            @pl.when(jnp.logical_not(joined))
            def _():
                hand_to(ret, rr)

            return carry

        lax.fori_loop(0, local, hand, 0)

    tile = 256
    inner_tiles = [slice(n, n + tile) for n in range(0, hidden.shape[4], tile)]
    out_width = downv.shape[1] // gates

    def expert(j, c):
        with jax.named_scope("wait_inc"):
            copied(inc.at[j, c], inc.at[j, c], pr.at[j, c]).wait()
        taken_in = inc[j, c].reshape(SIDES * capacity, share)
        for cols in inner_tiles:
            acc = jnp.dot(taken_in, upv[c, :, cols], preferred_element_type=f32)
            acc = acc.reshape(SIDES, PARTS, few, tile)

            @pl.when(c == 0)
            def _():
                hidden[j, :, :, :, cols] = acc

            @pl.when(c != 0)
            def _():
                hidden[j, :, :, :, cols] += acc

        @pl.when(c == chunks - 1)
        def _():
            active = jnp.maximum(hidden[j], 0.0).astype(bf16).reshape(SIDES * capacity, -1)
            for k in range(gates):
                obuf[j, k] = (
                    jnp.dot(
                        active,
                        downv[:, k * out_width : (k + 1) * out_width],
                        preferred_element_type=f32,
                    )
                    .astype(bf16)
                    .reshape(SIDES, PARTS, few, out_width)
                )
            with jax.named_scope("back"):
                give_back(j, None)

    def expert_part(j, part):
        c = chunks - 1
        with jax.named_scope("wait_part"):
            arriving = inc.at[j, c, :, part]
            copied(arriving, arriving, ph.at[part]).wait()
        taken_in = inc[j, c, :, part].reshape(SIDES * few, share)
        active = []
        for cols in inner_tiles:
            acc = jnp.dot(taken_in, upv[c, :, cols], preferred_element_type=f32)
            acc += hidden[j, :, part, :, cols].reshape(SIDES * few, tile)
            active.append(jnp.maximum(acc, 0.0).astype(bf16))
        active = jnp.concatenate(active, axis=1)
        for k in range(gates):
            obuf[j, k, :, part] = (
                jnp.dot(
                    active,
                    downv[:, k * out_width : (k + 1) * out_width],
                    preferred_element_type=f32,
                )
                .astype(bf16)
                .reshape(SIDES, few, out_width)
            )
        with jax.named_scope("back"):
            give_back(j, part)

    def gate_logits():
        partial = 0.0
        for c in range(chunks):
            partial += lax.dot_general(
                gatev[:, c * width : (c + 1) * width],
                blocks[z, c],
                (((1,), (1,)), ((), ())),
                preferred_element_type=f32,
            )
        logits[g] = partial
        for copy in gate_routes:
            copy.start()

    def gate_factor():
        with jax.named_scope("wait_gate"):
            for copy in gate_routes:
                copy.wait_recv()
        summed = logits[0]
        for k in range(1, gates):
            summed += logits[k]
        top = jnp.max(summed, axis=0, keepdims=True)
        terms = jnp.exp(summed - top)
        scale = mask[...].astype(f32).reshape(1, rows) / jnp.sum(terms, axis=0, keepdims=True)
        factor[...] = total * terms * scale

        @pl.when(edge)
        def _():
            edge_route.start()

    def join(j, p, weight, returned, sem, index, first):
        ranks = lax.broadcasted_iota(jnp.int32, (capacity, rows), 0).astype(f32)

        def one(i, carry):
            line = places[j, pl.ds(p * local + i, 1), :]
            scale = weight[pl.ds(p * local + i, 1), :]
            select[pl.ds(pl.multiple_of(i * capacity, capacity), capacity), :] = jnp.where(
                line == ranks, scale, 0.0
            ).astype(bf16)
            return carry

        lax.fori_loop(0, local, one, 0)
        with jax.named_scope("wait_ret"):
            copied(returned.at[p], returned.at[p], sem.at[p]).wait()
        found = lax.dot_general(
            select[...],
            returned[p].reshape(slots, out_width),
            (((0,), (0,)), ((), ())),
            preferred_element_type=f32,
        )

        @pl.when(first)
        def _():
            mixed[index] = found

        @pl.when(jnp.logical_not(first))
        def _():
            mixed[index] += found

    def job(t, carry):
        code = jnp.where(edge, table(EDGE_JOBS, t), table(MIDDLE_JOBS, t))
        kind, rel, c = code // 16, lax.rem(code // 4, 4), lax.rem(code, 4)
        j = plane_of(rel)

        @pl.when(kind == WAIT)
        def _():
            wait(j, rel, c)

        @pl.when((kind == END) | (kind == LOCAL))
        def _():
            dispatch(j, rel, c, kind == END)

        @pl.when(kind == EXPERT)
        def _():
            expert(j, c)

        @pl.when(kind == END_PART)
        def _():
            dispatch_part(c)

        @pl.when(kind == EXPERT_PART)
        def _():
            expert_part(j, c)

        @pl.when(kind == WEIGHTS)
        def _():
            with jax.named_scope("wait_w"):
                for copy in weights:
                    copy.wait()

        @pl.when(kind == LOGITS)
        def _():
            gate_logits()

        @pl.when(kind == FACTOR)
        def _():
            gate_factor()

        @pl.when(kind == JOIN_EDGE)
        def _():
            @pl.when(rel == OWN)
            def _():
                copied(edge_factor, edge_factor, fr).wait()

            join(near, j, edge_factor, edge_ret, er, 0, rel == OWN)

            @pl.when(rel == FAR)
            def _():
                part[...] = mixed[0].astype(bf16)
                part_route.start()

        @pl.when(kind == JOIN)
        def _():
            join(z, j, factor, ret, rr, 1, edge | (rel == OWN))

        return carry

    lax.fori_loop(0, jnp.where(edge, len(EDGE_JOBS), len(MIDDLE_JOBS)), job, 0)

    @pl.when(edge)
    def _():
        with jax.named_scope("wait_taken"):
            copied(taken, taken, tr).wait()
        out[...] = (mixed[1] + taken[...].astype(f32)).astype(bf16)

    @pl.when(middle)
    def _():
        out[...] = mixed[1].astype(bf16)

    for copy in gate_routes:
        copy.wait_send()
    ids_on(z, id_s.at[0]).wait_send()
    for c in range(chunks):
        shift(z, c).wait_send()
    within = dbuf.at[EDGE, :, :, pl.ds(0, local - 1)]
    copied(within, within, ds).wait()
    handed = ret.at[pl.ds(0, planes - 1)]
    few_more = ret.at[0, pl.ds(0, local - 2)]
    one_more = ret.at[0, 0]
    copied(handed, handed, rs).wait()
    copied(few_more, few_more, rs).wait()

    @pl.when(edge)
    def _():
        copied(one_more, one_more, rs).wait()
        edge_route.wait_send()

    @pl.when(middle)
    def _():
        part_route.wait_send()
        ids_on(near, id_s.at[1]).wait_send()
        for c in range(chunks):
            shift(near, c).wait_send()
        others = dbuf.at[pl.ds(0, planes - 1), :, :, pl.ds(0, local - 1)]
        copied(others, others, ds).wait()
        ahead = dbuf.at[pl.ds(planes, planes - 1)]
        copied(ahead, ahead, ds).wait()


def exchange(samples, ids, pads, gate_weight, up, down, planes, gates, capacity):
    rows, share = samples.shape
    local = SIDES * gates
    total = planes * local
    width = share // CHUNKS
    depth, inner = up.shape[1:]
    outer = down.shape[2]
    out_width = outer // gates
    bf16, f32 = jnp.bfloat16, jnp.float32
    dma = pltpu.SemaphoreType.DMA
    hbm = pl.BlockSpec(memory_space=pl.ANY)
    slots = local * capacity
    few = capacity // PARTS
    kinds = 2 * planes - 1
    return pl.pallas_call(
        functools.partial(exchange_kernel, gates, capacity),
        out_shape=pltpu.VMEM((rows, out_width), bf16),
        in_specs=[hbm] * 6,
        out_specs=pl.BlockSpec(memory_space=pltpu.VMEM),
        scratch_shapes=[
            pltpu.VMEM((planes, CHUNKS, rows, width), bf16),
            pltpu.VMEM((planes,) + ids.shape, jnp.int32),
            pltpu.VMEM(pads.shape, jnp.int32),
            pltpu.VMEM(gate_weight.shape, bf16),
            pltpu.VMEM((planes, total, rows), f32),
            pltpu.VMEM((rows, rows), bf16),
            pltpu.VMEM((kinds, PARTS, local, few, rows), bf16),
            pltpu.VMEM((kinds, CHUNKS, PARTS, local, few, width), bf16),
            pltpu.VMEM((planes, CHUNKS, SIDES, PARTS, few, gates * width), bf16),
            pltpu.VMEM((CHUNKS, depth // CHUNKS, inner), bf16),
            pltpu.VMEM((inner, outer), bf16),
            pltpu.VMEM((planes, SIDES, PARTS, few, inner), f32),
            pltpu.VMEM((planes, gates, SIDES, PARTS, few, out_width), bf16),
            pltpu.VMEM((gates, total, rows), f32),
            pltpu.VMEM((total, rows), f32),
            pltpu.VMEM((total, rows), f32),
            pltpu.VMEM((planes, local, PARTS, few, out_width), bf16),
            pltpu.VMEM((planes, local, PARTS, few, out_width), bf16),
            pltpu.VMEM((slots, rows), bf16),
            pltpu.VMEM((2, rows, out_width), f32),
            pltpu.VMEM((rows, out_width), bf16),
            pltpu.VMEM((rows, out_width), bf16),
            dma((CHUNKS,)),
            dma((1 + CHUNKS * gates,)),
            dma((3,)),
            dma((planes, CHUNKS)),
            dma((planes, CHUNKS)),
            dma((2,)),
            dma((planes,)),
            dma,
            dma((planes, CHUNKS)),
            dma((PARTS,)),
            dma,
            dma((planes,)),
            dma((planes,)),
            dma((gates,)),
            dma((gates,)),
            dma,
            dma,
            dma,
            dma,
        ],
        compiler_params=pltpu.CompilerParams(
            collective_id=0, has_side_effects=True, vmem_limit_bytes=58 << 20
        ),
    )(samples, ids, pads, gate_weight, up, down)


def in_one_kernel(samples, gate_weight, expert_ids, pad_mask, up_weight, down_weight):
    group_count = lax.axis_size("expert")
    gate_count = lax.axis_size("gate")
    expert_count = group_count * gate_count
    return exchange(
        samples,
        expert_ids.T,
        pad_mask,
        gate_weight.T,
        up_weight,
        down_weight,
        group_count // SIDES,
        gate_count,
        4 * samples.shape[0] // expert_count,
    )


def fits(samples, up_weight, down_weight):
    group_count = lax.axis_size("expert")
    capacity = 4 * samples.shape[0] // (group_count * lax.axis_size("gate"))
    planes = group_count // SIDES
    held = 2 * (planes * samples.size * 3 + up_weight.size + down_weight.size)
    return planes == 4 and group_count % SIDES == 0 and capacity % (16 * PARTS) == 0 and held < 40 << 20


def per_device(samples, gate_weight, expert_ids, pad_mask, up_weight, down_weight):
    if fits(samples, up_weight, down_weight):
        return in_one_kernel(
            samples, gate_weight, expert_ids, pad_mask, up_weight, down_weight
        )
    row_count, share = samples.shape
    group_count = lax.axis_size("expert")
    gate_count = lax.axis_size("gate")
    expert_count = group_count * gate_count
    capacity = 4 * row_count // expert_count
    partial = jnp.dot(samples, gate_weight, preferred_element_type=jnp.float32)
    logits = jnp.sum(lax.all_gather(partial, "gate"), axis=0)
    first, second, member, before = routing(expert_ids, expert_count)
    place = jnp.where(member, before, -1).T
    ranks = jnp.arange(capacity, dtype=jnp.int32)
    send = (place[:, None, :] == ranks[None, :, None]).astype(jnp.bfloat16)
    outgoing = jnp.dot(
        send.reshape(expert_count * capacity, row_count), samples, preferred_element_type=jnp.float32
    ).astype(jnp.bfloat16)
    incoming = lax.all_to_all(
        outgoing.reshape(expert_count, capacity, share),
        ("expert", "gate"),
        split_axis=0,
        concat_axis=0,
        tiled=True,
    ).reshape(group_count, gate_count, capacity, share)
    hidden = 0.0
    for g in range(gate_count):
        hidden += jnp.dot(
            incoming[:, g].reshape(group_count * capacity, share),
            up_weight[0, g * share : (g + 1) * share],
            preferred_element_type=jnp.float32,
        )
    active = jnp.maximum(hidden, 0.0).astype(jnp.bfloat16)
    expert_out = jnp.dot(active, down_weight[0], preferred_element_type=jnp.float32).astype(
        jnp.bfloat16
    )
    out_share = expert_out.shape[1] // gate_count
    outbound = expert_out.reshape(group_count, capacity, gate_count, out_share)
    outbound = outbound.transpose(0, 2, 1, 3).reshape(expert_count, capacity, out_share)
    returned = lax.all_to_all(
        outbound, ("expert", "gate"), split_axis=0, concat_axis=0, tiled=True
    ).reshape(expert_count * capacity, out_share)
    factor0, factor1 = factors(logits, first, second, pad_mask, expert_count)
    slots = jnp.arange(expert_count * capacity, dtype=jnp.int32)[None, :]
    mixed = 0.0
    for k, (chosen, factor) in enumerate(((first, factor0), (second, factor1))):
        rank = jnp.sum(jnp.where(chosen, before, 0), axis=1, keepdims=True)
        position = expert_ids[:, k : k + 1] * capacity + rank
        pick = (position == slots).astype(jnp.bfloat16)
        mixed += factor * jnp.dot(pick, returned, preferred_element_type=jnp.float32)
    return mixed.astype(jnp.bfloat16)


def solution(mesh):
    placed = (
        P("expert", "gate"),
        P("gate", None),
        P("expert", None),
        P("expert"),
        P(("expert", "gate"), None, None),
        P(("expert", "gate"), None, None),
    )
    return jax.shard_map(
        per_device, mesh=mesh, in_specs=placed, out_specs=P("expert", "gate"), check_vma=False
    )
```

time: 135 us -> 121 us (0.90)
  the two profiles are of different devices: /device:TPU:15 before, /device:TPU:0 now
where the time goes in v2:
time: 121 us; the launch traced here: 119 us
  Pallas kernels  119 us (98%)
    pallas_call x1, Pallas kernels, exchange(): pl.pallas_call(functools.partial(exchange_kernel, gates, capacity), out_s...  119 us

profile of v2, /device:TPU:0, one launch (start us, length us, event | category | flops | bytes accessed | tf_op | source)
XLA Modules:
  0.0 119.3 jit_solution(13226392382774332125)
XLA Ops:
  0.0 118.6 %shard_map.64 = bf16[768,256]{1,0:T(8,128)(2,1)S(1)} custom-call(bf16[768,1024]{1,0:T(8,128)(2,1)} %samples.1, s32[2,768]{1,0:T(2,128)} %bitcast.3, s32[768]{0:T(1024)} %pads.1, bf16[32,1024]{1,0:T(8,128)(2,1)} %bitcast.2, bf16[1,4096,1024]{2,1,0:T(8,128)(2,1)} %up.1, bf16[1,1024,1024]{2,1,0:T(8,128)(2,1)} %down.1), custom_call_target="tpu_custom_call" | custom-call | tf_op jit(solution)/shard_map/pallas_call | solution.py:704
  118.6 0.7 copy.8

commit v3 on v2

--- a/solution.py
+++ b/solution.py
@@ -11,7 +11,8 @@
 MESH = pl.DeviceIdType.MESH
 CHUNKS = 4
 SIDES = 2
-PARTS = 2
+PARTS = 3
+STRIDE = 5
 
 
 def routing(expert_ids, expert_count):
@@ -58,7 +59,7 @@
     return out
 
 
-NONE, WAIT, END, LOCAL, EXPERT, LOGITS, FACTOR, JOIN_EDGE, JOIN, END_PART, EXPERT_PART, WEIGHTS = range(12)
+NONE, WAIT, END, LOCAL, EXPERT, LOGITS, FACTOR, JOIN_EDGE, JOIN, END_PART, EXPERT_PART, WEIGHTS, BACK = range(13)
 OWN, EDGE, INNER, FAR = range(4)
 
 
@@ -119,14 +120,19 @@
     (LOCAL, INNER, 2),
     (EXPERT, FAR, 2),
     (EXPERT, FAR, 3),
+    (BACK, FAR, 0),
     (WAIT, INNER, 3),
     (END, INNER, 3),
     (LOCAL, INNER, 3),
     (END, OWN, 2),
     (END_PART, OWN, 0),
     (END_PART, OWN, 1),
+    (END_PART, OWN, 2),
+    (BACK, EDGE, 0),
+    (BACK, OWN, 0),
     (EXPERT, INNER, 2),
     (EXPERT, INNER, 3),
+    (BACK, INNER, 0),
     (JOIN_EDGE, OWN, 0),
     (JOIN_EDGE, INNER, 0),
     (JOIN_EDGE, FAR, 0),
@@ -149,17 +155,21 @@
     (EXPERT, EDGE, 2),
     (EXPERT, OWN, 1),
     (EXPERT, EDGE, 3),
+    (BACK, EDGE, 0),
     (EXPERT, INNER, 0),
     (EXPERT, INNER, 1),
     (EXPERT, FAR, 0),
     (EXPERT, FAR, 1),
     (EXPERT, FAR, 2),
     (EXPERT, FAR, 3),
+    (BACK, FAR, 0),
     (EXPERT, INNER, 2),
     (EXPERT, INNER, 3),
+    (BACK, INNER, 0),
     (EXPERT, OWN, 2),
     (EXPERT_PART, OWN, 0),
     (EXPERT_PART, OWN, 1),
+    (EXPERT_PART, OWN, 2),
     (JOIN, EDGE, 0),
 )
 
@@ -317,68 +327,6 @@
 
         build(rel, z)
 
-    with jax.named_scope("inputs"):
-        for copy in inputs:
-            copy.wait()
-    with jax.named_scope("prepare"):
-        prepare(z, jnp.where(edge, EDGE, OWN))
-    with jax.named_scope("samples"):
-        for copy in own:
-            copy.wait()
-    with jax.named_scope("barrier"):
-        pl.semaphore_wait(barrier, greeted)
-
-    def ids_on(j, sem):
-        return sent(named.at[j], named.at[j], sem, id_r.at[j], at(inner, mine))
-
-    def shift(j, c):
-        return sent(
-            blocks.at[j, c], blocks.at[j, c], raw_s.at[j, c], raw_r.at[j, c], at(inner, mine)
-        )
-
-    ids_on(z, id_s.at[0]).start()
-    for c in range(2):
-        shift(z, c).start()
-
-    @pl.when(edge)
-    def _():
-        for c in range(2, chunks):
-            shift(z, c).start()
-
-    for copy in weights:
-        copy.start()
-    gate_routes = []
-    for d in range(1, gates):
-        t = lax.rem(g + d, gates)
-        gate_routes.append(sent(logits.at[g], logits.at[g], gs.at[d - 1], gr.at[d - 1], (e, t)))
-    edge_route = sent(factor, edge_factor, fs, fr, at(inner, mine))
-    part_route = sent(part, taken, ts, tr, at(near, mine))
-
-    def wait(j, rel, c):
-        with jax.named_scope("wait_raw"):
-            copied(blocks.at[j, c], blocks.at[j, c], raw_r.at[j, c]).wait()
-
-        @pl.when(c == 0)
-        def _():
-            copied(named.at[j], named.at[j], id_r.at[j]).wait()
-
-        @pl.when(rel == EDGE)
-        def _():
-            @pl.when(c == 0)
-            def _():
-                ids_on(j, id_s.at[1]).start()
-
-            shift(j, c).start()
-
-            @pl.when(c == chunks - 1)
-            def _():
-                for k in range(2, chunks):
-                    shift(z, k).start()
-
-        @pl.when(c == 0)
-        def _():
-            prepare(j, rel)
-
     def pick(index, part, j, c):
         dbuf[index, c, part] = (
             jnp.dot(
@@ -390,15 +338,82 @@
             .reshape(local, few, width)
         )
 
-    def dispatch(j, rel, c, to_end):
+    with jax.named_scope("inputs"):
+        for copy in inputs:
+            copy.wait()
+    with jax.named_scope("prepare"):
+        prepare(z, jnp.where(edge, EDGE, OWN))
+    with jax.named_scope("samples"):
+        for copy in own:
+            copy.wait()
+    for q in range(PARTS):
+        pick(jnp.where(edge, EDGE, planes), q, z, 0)
+    with jax.named_scope("barrier"):
+        pl.semaphore_wait(barrier, greeted)
+
+    def ids_on(j, sem):
+        return sent(named.at[j], named.at[j], sem, id_r.at[j], at(inner, mine))
+
+    def shift(j, c):
+        return sent(
+            blocks.at[j, c], blocks.at[j, c], raw_s.at[j, c], raw_r.at[j, c], at(inner, mine)
+        )
+
+    ids_on(z, id_s.at[0]).start()
+    for c in range(2):
+        shift(z, c).start()
+
+    @pl.when(edge)
+    def _():
+        for c in range(2, chunks):
+            shift(z, c).start()
+
+    for copy in weights:
+        copy.start()
+    gate_routes = []
+    for d in range(1, gates):
+        t = lax.rem(g + d, gates)
+        gate_routes.append(sent(logits.at[g], logits.at[g], gs.at[d - 1], gr.at[d - 1], (e, t)))
+    edge_route = sent(factor, edge_factor, fs, fr, at(inner, mine))
+    part_route = sent(part, taken, ts, tr, at(near, mine))
+
+    def wait(j, rel, c):
+        with jax.named_scope("wait_raw"):
+            copied(blocks.at[j, c], blocks.at[j, c], raw_r.at[j, c]).wait()
+
+        @pl.when(c == 0)
+        def _():
+            copied(named.at[j], named.at[j], id_r.at[j]).wait()
+
+        @pl.when(rel == EDGE)
+        def _():
+            @pl.when(c == 0)
+            def _():
+                ids_on(j, id_s.at[1]).start()
+
+            shift(j, c).start()
+
+            @pl.when(c == chunks - 1)
+            def _():
+                for k in range(2, chunks):
+                    shift(z, k).start()
+
+        @pl.when(c == 0)
+        def _():
+            prepare(j, rel)
+
+    def dispatch(j, rel, c, to_end, fresh):
         index = jnp.where(to_end, end_index(rel), rel)
         plane = jnp.where(to_end, near, z)
-        with jax.named_scope("pick"):
-            for part in range(PARTS):
-                pick(index, part, j, c)
+
+        @pl.when(fresh)
+        def _():
+            with jax.named_scope("pick"):
+                for part in range(PARTS):
+                    pick(index, part, j, c)
 
         def give(d, carry):
-            i = lax.rem(mine + d, local)
+            i = lax.rem(mine + STRIDE * d, local)
             piece = dbuf.at[index, c, :, i]
             place = inc.at[j, c, y, :, :, pl.ds(g * width, width)]
             here = jnp.logical_not(to_end) & (d == 0)
@@ -420,7 +435,7 @@
         pick(planes, part, z, c)
 
         def give(d, carry):
-            i = lax.rem(mine + d, local)
+            i = lax.rem(mine + STRIDE * d, local)
             sent(
                 dbuf.at[planes, c, part, i],
                 inc.at[z, c, y, part, :, pl.ds(g * width, width)],
@@ -488,21 +503,20 @@
             def _():
                 hidden[j, :, :, :, cols] += acc
 
-        @pl.when(c == chunks - 1)
-        def _():
-            active = jnp.maximum(hidden[j], 0.0).astype(bf16).reshape(SIDES * capacity, -1)
-            for k in range(gates):
-                obuf[j, k] = (
-                    jnp.dot(
-                        active,
-                        downv[:, k * out_width : (k + 1) * out_width],
-                        preferred_element_type=f32,
-                    )
-                    .astype(bf16)
-                    .reshape(SIDES, PARTS, few, out_width)
+    def project(j):
+        active = jnp.maximum(hidden[j], 0.0).astype(bf16).reshape(SIDES * capacity, -1)
+        for k in range(gates):
+            obuf[j, k] = (
+                jnp.dot(
+                    active,
+                    downv[:, k * out_width : (k + 1) * out_width],
+                    preferred_element_type=f32,
                 )
-            with jax.named_scope("back"):
-                give_back(j, None)
+                .astype(bf16)
+                .reshape(SIDES, PARTS, few, out_width)
+            )
+        with jax.named_scope("back"):
+            give_back(j, None)
 
     def expert_part(j, part):
         c = chunks - 1
@@ -598,11 +612,15 @@
 
         @pl.when((kind == END) | (kind == LOCAL))
         def _():
-            dispatch(j, rel, c, kind == END)
+            dispatch(j, rel, c, kind == END, t > 0)
 
         @pl.when(kind == EXPERT)
         def _():
             expert(j, c)
+
+        @pl.when(kind == BACK)
+        def _():
+            project(j)
 
         @pl.when(kind == END_PART)
         def _():

time: 121 us -> 119 us (0.983)
  no operation moved by 1% of the time
where the time goes in v3:
time: 119 us; the launch traced here: 118 us
  Pallas kernels  118 us (99%)
    pallas_call x1, Pallas kernels, exchange(): pl.pallas_call(functools.partial(exchange_kernel, gates, capacity), out_s...  118 us

profile of v3, /device:TPU:0, one launch (start us, length us, event | category | flops | bytes accessed | tf_op | source)
XLA Modules:
  0.0 118.5 jit_solution(13316692509990940661)
XLA Ops:
  0.0 117.7 %shard_map.64 = bf16[768,256]{1,0:T(8,128)(2,1)S(1)} custom-call(bf16[768,1024]{1,0:T(8,128)(2,1)} %samples.1, s32[2,768]{1,0:T(2,128)} %bitcast.3, s32[768]{0:T(1024)} %pads.1, bf16[32,1024]{1,0:T(8,128)(2,1)} %bitcast.2, bf16[1,4096,1024]{2,1,0:T(8,128)(2,1)} %up.1, bf16[1,1024,1024]{2,1,0:T(8,128)(2,1)} %down.1), custom_call_target="tpu_custom_call" | custom-call | tf_op jit(solution)/shard_map/pallas_call | solution.py:722
  117.7 0.7 copy.8

commit v4 on v3

--- a/solution.py
+++ b/solution.py
@@ -59,7 +59,7 @@
     return out
 
 
-NONE, WAIT, END, LOCAL, EXPERT, LOGITS, FACTOR, JOIN_EDGE, JOIN, END_PART, EXPERT_PART, WEIGHTS, BACK = range(13)
+NONE, WAIT, END, LOCAL, EXPERT, LOGITS, FACTOR, JOIN_EDGE, JOIN, END_PART, EXPERT_PART, WEIGHTS, BACK, SETTLE = range(14)
 OWN, EDGE, INNER, FAR = range(4)
 
 
@@ -68,7 +68,6 @@
 
 
 MIDDLE_JOBS = coded(
-    (END, OWN, 0),
     (LOGITS, OWN, 0),
     (LOCAL, OWN, 0),
     (LOCAL, OWN, 1),
@@ -139,10 +138,10 @@
     (JOIN, OWN, 0),
     (JOIN, INNER, 0),
     (JOIN, FAR, 0),
+    (SETTLE, OWN, 0),
     (JOIN, EDGE, 0),
 )
 EDGE_JOBS = coded(
-    (LOCAL, EDGE, 0),
     (LOGITS, EDGE, 0),
     (LOCAL, EDGE, 1),
     (LOCAL, EDGE, 2),
@@ -171,6 +170,7 @@
     (EXPERT_PART, OWN, 1),
     (EXPERT_PART, OWN, 2),
     (JOIN, EDGE, 0),
+    (SETTLE, OWN, 0),
 )
 
 
@@ -258,20 +258,6 @@
 
     barrier = pltpu.get_barrier_semaphore()
 
-    def greet(d, carry):
-        plane = z - 1 + d // local
-        i = lax.rem(mine + d, local)
-
-        @pl.when((plane >= 0) & (plane < planes) & (d != local))
-        def _():
-            pl.semaphore_signal(barrier, inc=1, device_id=at(plane, i), device_id_type=MESH)
-
-        return carry
-
-    with jax.named_scope("greet"):
-        lax.fori_loop(0, 3 * local, greet, 0)
-    greeted = jnp.where(edge, 2, 3) * local - 1
-
     inputs = (
         copied(ids, named.at[z], in_sem.at[0]),
         copied(pads, mask, in_sem.at[1]),
@@ -285,6 +271,20 @@
     ]
     for copy in own:
         copy.start()
+    def greet(d, carry):
+        plane = z + table((toward, -toward, 0), d // local)
+        i = lax.rem(mine + d, local)
+
+        @pl.when((plane >= 0) & (plane < planes) & (d != 2 * local))
+        def _():
+            pl.semaphore_signal(barrier, inc=1, device_id=at(plane, i), device_id_type=MESH)
+
+        return carry
+
+    with jax.named_scope("greet"):
+        lax.fori_loop(0, 3 * local, greet, 0)
+    greeted = jnp.where(edge, 2, 3) * local - 1
+
     weights = [copied(down.at[0], downv, w_sem.at[0])]
     for c in range(chunks):
         for k in range(gates):
@@ -292,7 +292,7 @@
                 copied(
                     up.at[0, pl.ds(k * share + c * width, width)],
                     upv.at[c, pl.ds(k * width, width)],
-                    w_sem.at[1 + c * gates + k],
+                    w_sem.at[1],
                 )
             )
 
@@ -304,28 +304,23 @@
     def end_index(rel):
         return jnp.where(rel == OWN, planes, planes - 1 + rel)
 
-    def prepare(j, rel):
+    def locate(j):
         lanes = lax.broadcasted_iota(jnp.int32, (total, rows), 0)
         member = (named[j, 0:1, :] == lanes) | (named[j, 1:2, :] == lanes)
         flags = jnp.where(member, 1.0, 0.0).astype(bf16)
         before = jnp.dot(flags, lower[...], preferred_element_type=f32)
         places[j] = jnp.where(member, before, -1.0)
+
+    def build(j, index, plane):
         ranks = lax.broadcasted_iota(jnp.int32, (capacity, rows), 0).astype(f32)
 
-        def build(index, plane):
-            def one(i, carry):
-                line = places[j, pl.ds(plane * local + i, 1), :]
-                found = jnp.where(line == ranks, 1.0, 0.0).astype(bf16)
-                onehot[index, :, i] = found.reshape(PARTS, few, rows)
-                return carry
-
-            lax.fori_loop(0, local, one, 0)
-
-        @pl.when(middle & (rel != EDGE))
-        def _():
-            build(end_index(rel), near)
-
-        build(rel, z)
+        def one(i, carry):
+            line = places[j, pl.ds(plane * local + i, 1), :]
+            found = jnp.where(line == ranks, 1.0, 0.0).astype(bf16)
+            onehot[index, :, i] = found.reshape(PARTS, few, rows)
+            return carry
+
+        lax.fori_loop(0, local, one, 0)
 
     def pick(index, part, j, c):
         dbuf[index, c, part] = (
@@ -338,25 +333,50 @@
             .reshape(local, few, width)
         )
 
+    def hand_out(j, rel, c, to_end):
+        index = jnp.where(to_end, end_index(rel), rel)
+        plane = jnp.where(to_end, near, z)
+
+        def give(d, carry):
+            i = lax.rem(mine + STRIDE * d, local)
+            piece = dbuf.at[index, c, :, i]
+            place = inc.at[j, c, y, :, :, pl.ds(g * width, width)]
+            here = jnp.logical_not(to_end) & (d == 0)
+
+            @pl.when(here)
+            def _():
+                copied(piece, place, pr.at[j, c]).start()
+
+            @pl.when(jnp.logical_not(here))
+            def _():
+                sent(piece, place, ds, pr.at[j, c], at(plane, i)).start()
+
+            return carry
+
+        lax.fori_loop(0, local, give, 0)
+
     with jax.named_scope("inputs"):
         for copy in inputs:
             copy.wait()
+    first = jnp.where(edge, EDGE, planes)
     with jax.named_scope("prepare"):
-        prepare(z, jnp.where(edge, EDGE, OWN))
+        locate(z)
+        build(z, first, near)
     with jax.named_scope("samples"):
         for copy in own:
             copy.wait()
     for q in range(PARTS):
-        pick(jnp.where(edge, EDGE, planes), q, z, 0)
+        pick(first, q, z, 0)
     with jax.named_scope("barrier"):
         pl.semaphore_wait(barrier, greeted)
+    hand_out(z, jnp.where(edge, EDGE, OWN), 0, middle)
 
     def ids_on(j, sem):
         return sent(named.at[j], named.at[j], sem, id_r.at[j], at(inner, mine))
 
     def shift(j, c):
         return sent(
-            blocks.at[j, c], blocks.at[j, c], raw_s.at[j, c], raw_r.at[j, c], at(inner, mine)
+            blocks.at[j, c], blocks.at[j, c], raw_s, raw_r.at[j, c], at(inner, mine)
         )
 
     ids_on(z, id_s.at[0]).start()
@@ -370,6 +390,11 @@
 
     for copy in weights:
         copy.start()
+
+    @pl.when(middle)
+    def _():
+        build(z, OWN, z)
+
     gate_routes = []
     for d in range(1, gates):
         t = lax.rem(g + d, gates)
@@ -400,35 +425,20 @@
 
         @pl.when(c == 0)
         def _():
-            prepare(j, rel)
-
-    def dispatch(j, rel, c, to_end, fresh):
+            locate(j)
+
+            @pl.when(rel != EDGE)
+            def _():
+                build(j, end_index(rel), near)
+
+            build(j, rel, z)
+
+    def dispatch(j, rel, c, to_end):
         index = jnp.where(to_end, end_index(rel), rel)
-        plane = jnp.where(to_end, near, z)
-
-        @pl.when(fresh)
-        def _():
-            with jax.named_scope("pick"):
-                for part in range(PARTS):
-                    pick(index, part, j, c)
-
-        def give(d, carry):
-            i = lax.rem(mine + STRIDE * d, local)
-            piece = dbuf.at[index, c, :, i]
-            place = inc.at[j, c, y, :, :, pl.ds(g * width, width)]
-            here = jnp.logical_not(to_end) & (d == 0)
-
-            @pl.when(here)
-            def _():
-                copied(piece, place, pr.at[j, c]).start()
-
-            @pl.when(jnp.logical_not(here))
-            def _():
-                sent(piece, place, ds, pr.at[j, c], at(plane, i)).start()
-
-            return carry
-
-        lax.fori_loop(0, local, give, 0)
+        with jax.named_scope("pick"):
+            for part in range(PARTS):
+                pick(index, part, j, c)
+        hand_out(j, rel, c, to_end)
 
     def dispatch_part(part):
         c = chunks - 1
@@ -601,6 +611,23 @@
         def _():
             mixed[index] += found
 
+    def settle():
+        for copy in gate_routes:
+            copy.wait_send()
+        ids_on(z, id_s.at[0]).wait_send()
+        copied(blocks.at[z], blocks.at[z], raw_s).wait()
+        within = dbuf.at[EDGE, :, :, pl.ds(0, local - 1)]
+        copied(within, within, ds).wait()
+
+        @pl.when(middle)
+        def _():
+            ids_on(near, id_s.at[1]).wait_send()
+            copied(blocks.at[near], blocks.at[near], raw_s).wait()
+            others = dbuf.at[pl.ds(0, planes - 1), :, :, pl.ds(0, local - 1)]
+            copied(others, others, ds).wait()
+            ahead = dbuf.at[pl.ds(planes, planes - 1)]
+            copied(ahead, ahead, ds).wait()
+
     def job(t, carry):
         code = jnp.where(edge, table(EDGE_JOBS, t), table(MIDDLE_JOBS, t))
         kind, rel, c = code // 16, lax.rem(code // 4, 4), lax.rem(code, 4)
@@ -612,7 +639,7 @@
 
         @pl.when((kind == END) | (kind == LOCAL))
         def _():
-            dispatch(j, rel, c, kind == END, t > 0)
+            dispatch(j, rel, c, kind == END)
 
         @pl.when(kind == EXPERT)
         def _():
@@ -633,8 +660,8 @@
         @pl.when(kind == WEIGHTS)
         def _():
             with jax.named_scope("wait_w"):
-                for copy in weights:
-                    copy.wait()
+                weights[0].wait()
+                copied(upv, upv, w_sem.at[1]).wait()
 
         @pl.when(kind == LOGITS)
         def _():
@@ -656,6 +683,10 @@
             def _():
                 part[...] = mixed[0].astype(bf16)
                 part_route.start()
+
+        @pl.when(kind == SETTLE)
+        def _():
+            settle()
 
         @pl.when(kind == JOIN)
         def _():
@@ -669,19 +700,14 @@
     def _():
         with jax.named_scope("wait_taken"):
             copied(taken, taken, tr).wait()
-        out[...] = (mixed[1] + taken[...].astype(f32)).astype(bf16)
+        with jax.named_scope("fin_add"):
+            out[...] = (mixed[1] + taken[...].astype(f32)).astype(bf16)
 
     @pl.when(middle)
     def _():
-        out[...] = mixed[1].astype(bf16)
-
-    for copy in gate_routes:
-        copy.wait_send()
-    ids_on(z, id_s.at[0]).wait_send()
-    for c in range(chunks):
-        shift(z, c).wait_send()
-    within = dbuf.at[EDGE, :, :, pl.ds(0, local - 1)]
-    copied(within, within, ds).wait()
+        with jax.named_scope("fin_add"):
+            out[...] = mixed[1].astype(bf16)
+
     handed = ret.at[pl.ds(0, planes - 1)]
     few_more = ret.at[0, pl.ds(0, local - 2)]
     one_more = ret.at[0, 0]
@@ -696,13 +722,6 @@
     @pl.when(middle)
     def _():
         part_route.wait_send()
-        ids_on(near, id_s.at[1]).wait_send()
-        for c in range(chunks):
-            shift(near, c).wait_send()
-        others = dbuf.at[pl.ds(0, planes - 1), :, :, pl.ds(0, local - 1)]
-        copied(others, others, ds).wait()
-        ahead = dbuf.at[pl.ds(planes, planes - 1)]
-        copied(ahead, ahead, ds).wait()
 
 
 def exchange(samples, ids, pads, gate_weight, up, down, planes, gates, capacity):
@@ -748,9 +767,9 @@
             pltpu.VMEM((rows, out_width), bf16),
             pltpu.VMEM((rows, out_width), bf16),
             dma((CHUNKS,)),
-            dma((1 + CHUNKS * gates,)),
+            dma((2,)),
             dma((3,)),
-            dma((planes, CHUNKS)),
+            dma,
             dma((planes, CHUNKS)),
             dma((2,)),
             dma((planes,)),

time: 119 us -> 119 us (level)
  no operation moved by 1% of the time
where the time goes in v4:
time: 119 us
  Pallas kernels  118 us (99%)
    pallas_call x1, Pallas kernels, exchange(): pl.pallas_call(functools.partial(exchange_kernel, gates, capacity), out_s...  118 us

profile of v4, /device:TPU:0, one launch (start us, length us, event | category | flops | bytes accessed | tf_op | source)
XLA Modules:
  0.0 118.5 jit_solution(12808137361610126447)
XLA Ops:
  0.0 117.8 %shard_map.64 = bf16[768,256]{1,0:T(8,128)(2,1)S(1)} custom-call(bf16[768,1024]{1,0:T(8,128)(2,1)} %samples.1, s32[2,768]{1,0:T(2,128)} %bitcast.3, s32[768]{0:T(1024)} %pads.1, bf16[32,1024]{1,0:T(8,128)(2,1)} %bitcast.2, bf16[1,4096,1024]{2,1,0:T(8,128)(2,1)} %up.1, bf16[1,1024,1024]{2,1,0:T(8,128)(2,1)} %down.1), custom_call_target="tpu_custom_call" | custom-call | tf_op jit(solution)/shard_map/pallas_call | solution.py:741
  117.8 0.7 copy.8

commit v5 on v4

--- a/solution.py
+++ b/solution.py
@@ -59,7 +59,7 @@
     return out
 
 
-NONE, WAIT, END, LOCAL, EXPERT, LOGITS, FACTOR, JOIN_EDGE, JOIN, END_PART, EXPERT_PART, WEIGHTS, BACK, SETTLE = range(14)
+NONE, WAIT, END, LOCAL, EXPERT, LOGITS, FACTOR, JOIN_EDGE, JOIN, END_PART, EXPERT_PART, WEIGHTS, BACK, SETTLE, OPEN = range(15)
 OWN, EDGE, INNER, FAR = range(4)
 
 
@@ -70,6 +70,7 @@
 MIDDLE_JOBS = coded(
     (LOGITS, OWN, 0),
     (LOCAL, OWN, 0),
+    (OPEN, OWN, 0),
     (LOCAL, OWN, 1),
     (LOCAL, OWN, 2),
     (LOCAL, OWN, 3),
@@ -207,24 +208,15 @@
     part,
     taken,
     own_sem,
-    w_sem,
     in_sem,
-    raw_s,
+    ss,
     raw_r,
-    id_s,
     id_r,
-    ds,
     pr,
-    ph,
-    rs,
     rr,
     er,
-    gs,
     gr,
-    fs,
     fr,
-    ts,
-    tr,
 ):
     chunks = CHUNKS
     local = SIDES * gates
@@ -266,7 +258,7 @@
     for copy in inputs:
         copy.start()
     own = [
-        copied(samples.at[:, pl.ds(c * width, width)], blocks.at[z, c], own_sem.at[c])
+        copied(samples.at[:, pl.ds(c * width, width)], blocks.at[z, c], own_sem)
         for c in range(chunks)
     ]
     for copy in own:
@@ -275,7 +267,9 @@
         plane = z + table((toward, -toward, 0), d // local)
         i = lax.rem(mine + d, local)
 
-        @pl.when((plane >= 0) & (plane < planes) & (d != 2 * local))
+        told = (plane >= 0) & (plane < planes) & (d != 2 * local)
+
+        @pl.when(told & (edge | low | (plane != inner)))
         def _():
             pl.semaphore_signal(barrier, inc=1, device_id=at(plane, i), device_id_type=MESH)
 
@@ -283,16 +277,17 @@
 
     with jax.named_scope("greet"):
         lax.fori_loop(0, 3 * local, greet, 0)
-    greeted = jnp.where(edge, 2, 3) * local - 1
-
-    weights = [copied(down.at[0], downv, w_sem.at[0])]
+    greeted = jnp.where(edge | low, 2, 3) * local - 1
+    late = middle & low
+
+    weights = [copied(down.at[0], downv, in_sem.at[0])]
     for c in range(chunks):
         for k in range(gates):
             weights.append(
                 copied(
                     up.at[0, pl.ds(k * share + c * width, width)],
                     upv.at[c, pl.ds(k * width, width)],
-                    w_sem.at[1],
+                    own_sem,
                 )
             )
 
@@ -349,7 +344,7 @@
 
             @pl.when(jnp.logical_not(here))
             def _():
-                sent(piece, place, ds, pr.at[j, c], at(plane, i)).start()
+                sent(piece, place, ss, pr.at[j, c], at(plane, i)).start()
 
             return carry
 
@@ -363,25 +358,29 @@
         locate(z)
         build(z, first, near)
     with jax.named_scope("samples"):
-        for copy in own:
-            copy.wait()
+        copied(blocks.at[z], blocks.at[z], own_sem).wait()
     for q in range(PARTS):
         pick(first, q, z, 0)
     with jax.named_scope("barrier"):
         pl.semaphore_wait(barrier, greeted)
     hand_out(z, jnp.where(edge, EDGE, OWN), 0, middle)
 
-    def ids_on(j, sem):
-        return sent(named.at[j], named.at[j], sem, id_r.at[j], at(inner, mine))
+    def ids_on(j):
+        return sent(named.at[j], named.at[j], ss, id_r.at[j], at(inner, mine))
 
     def shift(j, c):
         return sent(
-            blocks.at[j, c], blocks.at[j, c], raw_s, raw_r.at[j, c], at(inner, mine)
+            blocks.at[j, c], blocks.at[j, c], ss, raw_r.at[j, c], at(inner, mine)
         )
 
-    ids_on(z, id_s.at[0]).start()
-    for c in range(2):
-        shift(z, c).start()
+    def open_inner():
+        ids_on(z).start()
+        for c in range(2):
+            shift(z, c).start()
+
+    @pl.when(jnp.logical_not(late))
+    def _():
+        open_inner()
 
     @pl.when(edge)
     def _():
@@ -398,15 +397,15 @@
     gate_routes = []
     for d in range(1, gates):
         t = lax.rem(g + d, gates)
-        gate_routes.append(sent(logits.at[g], logits.at[g], gs.at[d - 1], gr.at[d - 1], (e, t)))
-    edge_route = sent(factor, edge_factor, fs, fr, at(inner, mine))
-    part_route = sent(part, taken, ts, tr, at(near, mine))
+        gate_routes.append(sent(logits.at[g], logits.at[g], ss, gr, (e, t)))
+    edge_route = sent(factor, edge_factor, ss, fr, at(inner, mine))
+    part_route = sent(part, taken, ss, fr, at(near, mine))
 
     def wait(j, rel, c):
         with jax.named_scope("wait_raw"):
             copied(blocks.at[j, c], blocks.at[j, c], raw_r.at[j, c]).wait()
 
-        @pl.when(c == 0)
+        @pl.when((c == 0) & jnp.logical_not(late & (rel == INNER)))
         def _():
             copied(named.at[j], named.at[j], id_r.at[j]).wait()
 
@@ -414,7 +413,7 @@
         def _():
             @pl.when(c == 0)
             def _():
-                ids_on(j, id_s.at[1]).start()
+                ids_on(j).start()
 
             shift(j, c).start()
 
@@ -449,8 +448,8 @@
             sent(
                 dbuf.at[planes, c, part, i],
                 inc.at[z, c, y, part, :, pl.ds(g * width, width)],
-                ds,
-                ph.at[part],
+                ss,
+                raw_r.at[near, part],
                 at(near, i),
             ).start()
             return carry
@@ -479,7 +478,7 @@
 
                 @pl.when(jnp.logical_not(here))
                 def _():
-                    sent(block, spot, rs, sem.at[z], at(plane, i)).start()
+                    sent(block, spot, ss, sem.at[z], at(plane, i)).start()
 
             @pl.when(joined)
             def _():
@@ -532,7 +531,7 @@
         c = chunks - 1
         with jax.named_scope("wait_part"):
             arriving = inc.at[j, c, :, part]
-            copied(arriving, arriving, ph.at[part]).wait()
+            copied(arriving, arriving, raw_r.at[near, part]).wait()
         taken_in = inc[j, c, :, part].reshape(SIDES * few, share)
         active = []
         for cols in inner_tiles:
@@ -568,8 +567,8 @@
 
     def gate_factor():
         with jax.named_scope("wait_gate"):
-            for copy in gate_routes:
-                copy.wait_recv()
+            others = logits.at[pl.ds(0, gates - 1)]
+            copied(others, others, gr).wait()
         summed = logits[0]
         for k in range(1, gates):
             summed += logits[k]
@@ -612,21 +611,21 @@
             mixed[index] += found
 
     def settle():
-        for copy in gate_routes:
-            copy.wait_send()
-        ids_on(z, id_s.at[0]).wait_send()
-        copied(blocks.at[z], blocks.at[z], raw_s).wait()
+        others = logits.at[pl.ds(0, gates - 1)]
+        copied(others, others, ss).wait()
+        ids_on(z).wait_send()
+        copied(blocks.at[z], blocks.at[z], ss).wait()
         within = dbuf.at[EDGE, :, :, pl.ds(0, local - 1)]
-        copied(within, within, ds).wait()
+        copied(within, within, ss).wait()
 
         @pl.when(middle)
         def _():
-            ids_on(near, id_s.at[1]).wait_send()
-            copied(blocks.at[near], blocks.at[near], raw_s).wait()
-            others = dbuf.at[pl.ds(0, planes - 1), :, :, pl.ds(0, local - 1)]
-            copied(others, others, ds).wait()
+            ids_on(near).wait_send()
+            copied(blocks.at[near], blocks.at[near], ss).wait()
+            more = dbuf.at[pl.ds(0, planes - 1), :, :, pl.ds(0, local - 1)]
+            copied(more, more, ss).wait()
             ahead = dbuf.at[pl.ds(planes, planes - 1)]
-            copied(ahead, ahead, ds).wait()
+            copied(ahead, ahead, ss).wait()
 
     def job(t, carry):
         code = jnp.where(edge, table(EDGE_JOBS, t), table(MIDDLE_JOBS, t))
@@ -661,7 +660,7 @@
         def _():
             with jax.named_scope("wait_w"):
                 weights[0].wait()
-                copied(upv, upv, w_sem.at[1]).wait()
+                copied(upv, upv, own_sem).wait()
 
         @pl.when(kind == LOGITS)
         def _():
@@ -683,6 +682,11 @@
             def _():
                 part[...] = mixed[0].astype(bf16)
                 part_route.start()
+
+        @pl.when((kind == OPEN) & late)
+        def _():
+            copied(named.at[inner], named.at[inner], id_r.at[inner]).wait()
+            open_inner()
 
         @pl.when(kind == SETTLE)
         def _():
@@ -699,7 +703,7 @@
     @pl.when(edge)
     def _():
         with jax.named_scope("wait_taken"):
-            copied(taken, taken, tr).wait()
+            copied(taken, taken, fr).wait()
         with jax.named_scope("fin_add"):
             out[...] = (mixed[1] + taken[...].astype(f32)).astype(bf16)
 
@@ -711,12 +715,12 @@
     handed = ret.at[pl.ds(0, planes - 1)]
     few_more = ret.at[0, pl.ds(0, local - 2)]
     one_more = ret.at[0, 0]
-    copied(handed, handed, rs).wait()
-    copied(few_more, few_more, rs).wait()
+    copied(handed, handed, ss).wait()
+    copied(few_more, few_more, ss).wait()
 
     @pl.when(edge)
     def _():
-        copied(one_more, one_more, rs).wait()
+        copied(one_more, one_more, ss).wait()
         edge_route.wait_send()
 
     @pl.when(middle)
@@ -766,23 +770,14 @@
             pltpu.VMEM((2, rows, out_width), f32),
             pltpu.VMEM((rows, out_width), bf16),
             pltpu.VMEM((rows, out_width), bf16),
-            dma((CHUNKS,)),
-            dma((2,)),
+            dma,
             dma((3,)),
             dma,
             dma((planes, CHUNKS)),
-            dma((2,)),
             dma((planes,)),
-            dma,
             dma((planes, CHUNKS)),
-            dma((PARTS,)),
-            dma,
             dma((planes,)),
             dma((planes,)),
-            dma((gates,)),
-            dma((gates,)),
-            dma,
-            dma,
             dma,
             dma,
         ],

time: 119 us -> 117 us (0.983)
  Pallas kernels: 118 us -> 116 us
    pallas_call x1, Pallas kernels: 118 us -> 116 us  [exchange(): pl.pallas_call(functools.partial(exchange_kernel, gates, capacity), out_s...]
where the time goes in v5:
time: 117 us
  Pallas kernels  116 us (99%)
    pallas_call x1, Pallas kernels, exchange(): pl.pallas_call(functools.partial(exchange_kernel, gates, capacity), out_s...  116 us

profile of v5, /device:TPU:0, one launch (start us, length us, event | category | flops | bytes accessed | tf_op | source)
XLA Modules:
  0.0 117.1 jit_solution(3020960180195826533)
XLA Ops:
  0.0 116.3 %shard_map.64 = bf16[768,256]{1,0:T(8,128)(2,1)S(1)} custom-call(bf16[768,1024]{1,0:T(8,128)(2,1)} %samples.1, s32[2,768]{1,0:T(2,128)} %bitcast.3, s32[768]{0:T(1024)} %pads.1, bf16[32,1024]{1,0:T(8,128)(2,1)} %bitcast.2, bf16[1,4096,1024]{2,1,0:T(8,128)(2,1)} %up.1, bf16[1,1024,1024]{2,1,0:T(8,128)(2,1)} %down.1), custom_call_target="tpu_custom_call" | custom-call | tf_op jit(solution)/shard_map/pallas_call | solution.py:745
  116.4 0.7 copy.8

commit v6 on v5

--- a/solution.py
+++ b/solution.py
@@ -245,6 +245,9 @@
     def plane_of(rel):
         return table((mid, near, mid + toward, far), rel)
 
+    def row(j, reader):
+        return lax.rem(j - reader + planes, planes) - 1
+
     def at(plane, i):
         return (plane * SIDES + i // gates, lax.rem(i, gates))
 
@@ -263,11 +266,17 @@
     ]
     for copy in own:
         copy.start()
+    greeting = (
+        jnp.where(edge, toward, 0),
+        jnp.where(edge, 0, -toward),
+        jnp.where(edge, -toward, toward),
+    )
+
     def greet(d, carry):
-        plane = z + table((toward, -toward, 0), d // local)
+        plane = z + table(greeting, d // local)
         i = lax.rem(mine + d, local)
 
-        told = (plane >= 0) & (plane < planes) & (d != 2 * local)
+        told = (plane >= 0) & (plane < planes) & ((plane != z) | (i != mine))
 
         @pl.when(told & (edge | low | (plane != inner)))
         def _():
@@ -366,11 +375,11 @@
     hand_out(z, jnp.where(edge, EDGE, OWN), 0, middle)
 
     def ids_on(j):
-        return sent(named.at[j], named.at[j], ss, id_r.at[j], at(inner, mine))
+        return sent(named.at[j], named.at[j], ss, id_r.at[row(j, inner)], at(inner, mine))
 
     def shift(j, c):
         return sent(
-            blocks.at[j, c], blocks.at[j, c], ss, raw_r.at[j, c], at(inner, mine)
+            blocks.at[j, c], blocks.at[j, c], ss, raw_r.at[row(j, inner), c], at(inner, mine)
         )
 
     def open_inner():
@@ -403,11 +412,11 @@
 
     def wait(j, rel, c):
         with jax.named_scope("wait_raw"):
-            copied(blocks.at[j, c], blocks.at[j, c], raw_r.at[j, c]).wait()
+            copied(blocks.at[j, c], blocks.at[j, c], raw_r.at[row(j, z), c]).wait()
 
         @pl.when((c == 0) & jnp.logical_not(late & (rel == INNER)))
         def _():
-            copied(named.at[j], named.at[j], id_r.at[j]).wait()
+            copied(named.at[j], named.at[j], id_r.at[row(j, z)]).wait()
 
         @pl.when(rel == EDGE)
         def _():
@@ -449,7 +458,7 @@
                 dbuf.at[planes, c, part, i],
                 inc.at[z, c, y, part, :, pl.ds(g * width, width)],
                 ss,
-                raw_r.at[near, part],
+                raw_r.at[row(z, near), part],
                 at(near, i),
             ).start()
             return carry
@@ -474,11 +483,11 @@
 
                 @pl.when(here)
                 def _():
-                    copied(block, spot, sem.at[z]).start()
+                    copied(block, spot, sem).start()
 
                 @pl.when(jnp.logical_not(here))
                 def _():
-                    sent(block, spot, ss, sem.at[z], at(plane, i)).start()
+                    sent(block, spot, ss, sem, at(plane, i)).start()
 
             @pl.when(joined)
             def _():
@@ -486,7 +495,7 @@
 
             @pl.when(jnp.logical_not(joined))
             def _():
-                hand_to(ret, rr)
+                hand_to(ret, rr.at[z])
 
             return carry
 
@@ -531,7 +540,7 @@
         c = chunks - 1
         with jax.named_scope("wait_part"):
             arriving = inc.at[j, c, :, part]
-            copied(arriving, arriving, raw_r.at[near, part]).wait()
+            copied(arriving, arriving, raw_r.at[row(j, z), part]).wait()
         taken_in = inc[j, c, :, part].reshape(SIDES * few, share)
         active = []
         for cols in inner_tiles:
@@ -581,7 +590,7 @@
         def _():
             edge_route.start()
 
-    def join(j, p, weight, returned, sem, index, first):
+    def join(j, p, weight, returned, index, first):
         ranks = lax.broadcasted_iota(jnp.int32, (capacity, rows), 0).astype(f32)
 
         def one(i, carry):
@@ -593,8 +602,9 @@
             return carry
 
         lax.fori_loop(0, local, one, 0)
-        with jax.named_scope("wait_ret"):
-            copied(returned.at[p], returned.at[p], sem.at[p]).wait()
+        if returned is ret:
+            with jax.named_scope("wait_ret"):
+                copied(ret.at[p], ret.at[p], rr.at[p]).wait()
         found = lax.dot_general(
             select[...],
             returned[p].reshape(slots, out_width),
@@ -675,8 +685,10 @@
             @pl.when(rel == OWN)
             def _():
                 copied(edge_factor, edge_factor, fr).wait()
-
-            join(near, j, edge_factor, edge_ret, er, 0, rel == OWN)
+                joined = edge_ret.at[pl.ds(0, planes - 1)]
+                copied(joined, joined, er).wait()
+
+            join(near, j, edge_factor, edge_ret, 0, rel == OWN)
 
             @pl.when(rel == FAR)
             def _():
@@ -685,7 +697,7 @@
 
         @pl.when((kind == OPEN) & late)
         def _():
-            copied(named.at[inner], named.at[inner], id_r.at[inner]).wait()
+            copied(named.at[inner], named.at[inner], id_r.at[row(inner, z)]).wait()
             open_inner()
 
         @pl.when(kind == SETTLE)
@@ -694,7 +706,7 @@
 
         @pl.when(kind == JOIN)
         def _():
-            join(z, j, factor, ret, rr, 1, edge | (rel == OWN))
+            join(z, j, factor, ret, 1, edge | (rel == OWN))
 
         return carry
 
@@ -773,11 +785,11 @@
             dma,
             dma((3,)),
             dma,
+            dma((planes - 1, CHUNKS)),
+            dma((planes - 1,)),
             dma((planes, CHUNKS)),
             dma((planes,)),
-            dma((planes, CHUNKS)),
-            dma((planes,)),
-            dma((planes,)),
+            dma,
             dma,
             dma,
         ],

time: 117 us -> 117 us (level)
  no operation moved by 1% of the time
where the time goes in v6:
time: 117 us
  Pallas kernels  116 us (99%)
    pallas_call x1, Pallas kernels, exchange(): pl.pallas_call(functools.partial(exchange_kernel, gates, capacity), out_s...  116 us

profile of v6, /device:TPU:0, one launch (start us, length us, event | category | flops | bytes accessed | tf_op | source)
XLA Modules:
  0.0 116.9 jit_solution(15440406327198401839)
XLA Ops:
  0.0 116.2 %shard_map.64 = bf16[768,256]{1,0:T(8,128)(2,1)S(1)} custom-call(bf16[768,1024]{1,0:T(8,128)(2,1)} %samples.1, s32[2,768]{1,0:T(2,128)} %bitcast.3, s32[768]{0:T(1024)} %pads.1, bf16[32,1024]{1,0:T(8,128)(2,1)} %bitcast.2, bf16[1,4096,1024]{2,1,0:T(8,128)(2,1)} %up.1, bf16[1,1024,1024]{2,1,0:T(8,128)(2,1)} %down.1), custom_call_target="tpu_custom_call" | custom-call | tf_op jit(solution)/shard_map/pallas_call | solution.py:757
  116.2 0.7 copy.8

commit v7 on v6

--- a/solution.py
+++ b/solution.py
@@ -471,7 +471,7 @@
         plane = jnp.where(joined, jnp.where(j == 0, 1, planes - 2), j)
 
         def hand(d, carry):
-            i = lax.rem(mine + d, local)
+            i = lax.rem(mine + STRIDE * d, local)
             side, k = i // gates, lax.rem(i, gates)
             here = (plane == z) & (d == 0)
 

time: 117 us -> 117 us (level)
  no operation moved by 1% of the time
where the time goes in v7:
time: 117 us
  Pallas kernels  116 us (99%)
    pallas_call x1, Pallas kernels, exchange(): pl.pallas_call(functools.partial(exchange_kernel, gates, capacity), out_s...  116 us

profile of v7, /device:TPU:0, one launch (start us, length us, event | category | flops | bytes accessed | tf_op | source)
XLA Modules:
  0.0 116.9 jit_solution(14902398357749759485)
XLA Ops:
  0.0 116.2 %shard_map.64 = bf16[768,256]{1,0:T(8,128)(2,1)S(1)} custom-call(bf16[768,1024]{1,0:T(8,128)(2,1)} %samples.1, s32[2,768]{1,0:T(2,128)} %bitcast.3, s32[768]{0:T(1024)} %pads.1, bf16[32,1024]{1,0:T(8,128)(2,1)} %bitcast.2, bf16[1,4096,1024]{2,1,0:T(8,128)(2,1)} %up.1, bf16[1,1024,1024]{2,1,0:T(8,128)(2,1)} %down.1), custom_call_target="tpu_custom_call" | custom-call | tf_op jit(solution)/shard_map/pallas_call | solution.py:757
  116.2 0.7 copy.8
